TPU v7x, 256 devices: a whole 4x4x8 slice. The times are simulated.
256 devices in a mesh: seq: 4 (over x_hi, core), ctx: 8 (over z), head: 8 (over x_lo, y).
Axes of the slice: x: 4 (x_hi: 2, x_lo: 2; x = x_hi * 2 + x_lo), y: 4, z: 8, core: 2. Of those that a mesh axis runs over, the one named last changes fastest.
Arguments:
- stream: bfloat16 [4, 512, 2880], P('seq', 'ctx'), may hold values from -6 to 6
- query_weight: bfloat16 [2880, 4096], P(None, 'head'), may hold values from -0.109375 to 0.109375
- cache_keys: bfloat16 [4, 16384, 8, 64], P('seq', 'ctx', 'head'), may hold values from -1000 to 1000
- cache_values: bfloat16 [4, 16384, 8, 64], P('seq', 'ctx', 'head'), may hold values from -6 to 6
- new_keys: bfloat16 [4, 512, 8, 64], P('seq', 'ctx', 'head'), may hold values from -18 to 18
- new_values: bfloat16 [4, 512, 8, 64], P('seq', 'ctx', 'head'), may hold values from -6 to 6
- out_weight: bfloat16 [4096, 2880], P('head'), may hold values from -0.09375 to 0.09375
- norm_gain: float32 [2880], replicated, may hold values from 0.5 to 1.5
- expert_ids: int32 [4, 512, 4], P('seq', 'ctx'), may hold values from 0 to 31, all different within a row; in each aligned block of 64 rows (0 to 63, 64 to 127, ..., all dimensions but the last counted through in order) at most 16 rows name the same one
- expert_weights: float32 [4, 512, 4], P('seq', 'ctx'), may hold values from 0.1 to 1
- gate_weight: bfloat16 [32, 2880, 2880], P(('seq', 'ctx'), None, 'head'), may hold values from -0.109375 to 0.109375
- up_weight: bfloat16 [32, 2880, 2880], P(('seq', 'ctx'), None, 'head'), may hold values from -0.109375 to 0.109375
- down_weight: bfloat16 [32, 2880, 2880], P(('seq', 'ctx'), 'head'), may hold values from -0.109375 to 0.109375
Outputs:
- mixed: bfloat16 [4, 512, 2880], P('seq', 'ctx', 'head')
Inputs may be any that keep to these rules, and one draw needn't show every extreme that they name: `expert_ids`: in each aligned block of 64 rows (the tokens of one device) no expert is named by more than 16 rows; each row names 4 different experts.
All inputs are finite; a program needn't handle non-finite values.
Results may differ from a plain program's by a relative error of at most 0.015.
Values may be sent and summed in bfloat16 or wider, within the bound.
A program may use at most 64 MiB of HBM per device.

v0:
```python
import math

import jax
import jax.numpy as jnp
from jax import lax
from jax.sharding import PartitionSpec as P

CAP = 16


def sent_to_all(array, axis):
    copies = jnp.broadcast_to(array, (lax.axis_size(axis), *array.shape))
    return lax.all_to_all(copies, axis, split_axis=0, concat_axis=0, tiled=True)


def joined_along(tiles, dim):
    shape = list(tiles.shape[1:])
    shape[dim] *= tiles.shape[0]
    return jnp.moveaxis(tiles, 0, dim).reshape(shape)


def gathered_copies(array, axis, dim):
    tiles = sent_to_all(array, axis)
    return joined_along(tiles, dim)


def split_up(array, dim, count):
    before, after = (array.shape[:dim], array.shape[dim + 1 :])
    return jnp.moveaxis(array.reshape(*before, count, -1, *after), dim, 0)


def sent_and_summed(array, axis, dim):
    tiles = split_up(array, dim, lax.axis_size(axis))
    arrived = lax.all_to_all(tiles, axis, split_axis=0, concat_axis=0, tiled=True)
    return arrived.astype(jnp.float32).sum(axis=0)


def taken_together(array, axis):
    return sent_to_all(array, axis).sum(axis=0)


def body(
    stream,
    query_weight,
    cache_keys,
    cache_values,
    new_keys,
    new_values,
    out_weight,
    norm_gain,
    expert_ids,
    expert_weights,
    gate_weight,
    up_weight,
    down_weight,
):
    tokens = stream[0]
    count = tokens.shape[0]
    model = tokens.shape[1]
    kv_local = cache_keys.shape[2]
    head_dim = cache_keys.shape[3]
    group = query_weight.shape[1] // (kv_local * head_dim)
    cache_len = cache_keys.shape[1]
    height = count * group
    cycles = lax.axis_size("ctx")
    place = lax.axis_index("ctx")
    scale = 1.0 / math.sqrt(head_dim)
    query = jnp.dot(tokens, query_weight, preferred_element_type=jnp.float32).astype(jnp.bfloat16)
    query = (
        query.reshape(count, kv_local, group, head_dim)
        .transpose(1, 0, 2, 3)
        .reshape(kv_local, height, head_dim)
    )
    keys = jnp.concatenate([cache_keys[0], new_keys[0]], axis=0).transpose(1, 0, 2)
    values = jnp.concatenate([cache_values[0], new_values[0]], axis=0).transpose(1, 0, 2)
    extent = keys.shape[1]
    key_index = lax.broadcasted_iota(jnp.int32, (height, extent), 1)
    tok_index = lax.broadcasted_iota(jnp.int32, (height, extent), 0) // group
    fresh = key_index - cache_len
    blank = (
        jnp.full((kv_local, height), -jnp.inf, jnp.float32),
        jnp.zeros((kv_local, height), jnp.float32),
        jnp.zeros((kv_local, height, head_dim), jnp.float32),
    )

    def absorb(block, state, sources):
        top, total, numerator = state
        anchor = sources[:, None]
        allowed = (
            (key_index < cache_len) | (place < anchor) | (place == anchor) & (fresh <= tok_index)
        )
        scores = jnp.einsum("hrd,hkd->hrk", block, keys, preferred_element_type=jnp.float32) * scale
        scores = jnp.where(allowed[None], scores, -jnp.inf)
        new_top = jnp.max(scores, axis=-1)
        weights = jnp.exp(scores - new_top[..., None])
        fade = jnp.exp(top - new_top)
        total = total * fade + jnp.sum(weights, axis=-1)
        numerator = numerator * fade[..., None] + jnp.einsum(
            "hrk,hkd->hrd", weights.astype(jnp.bfloat16), values, preferred_element_type=jnp.float32
        )
        return (new_top, total, numerator)

    everyone = gathered_copies(query[None], "ctx", 0)

    def partial_state(operands):
        block, source = operands
        return absorb(block, blank, jnp.full((height,), source, jnp.int32))

    pieces = lax.map(partial_state, (everyone, lax.iota(jnp.int32, cycles)))
    tops, totals, numerators = lax.all_to_all(
        pieces, "ctx", split_axis=0, concat_axis=0, tiled=True
    )
    top = jnp.max(tops, axis=0)
    fade = jnp.exp(tops - top[None])
    total = jnp.sum(totals * fade, axis=0)
    numerator = jnp.sum(numerators * fade[..., None], axis=0)
    attn = (numerator / total[..., None]).astype(jnp.bfloat16)
    attn = (
        attn.reshape(kv_local, count, group, head_dim)
        .transpose(1, 0, 2, 3)
        .reshape(count, kv_local * group * head_dim)
    )
    projected = jnp.dot(attn, out_weight, preferred_element_type=jnp.float32)
    width = model // lax.axis_size("head")
    offset = lax.axis_index("head") * width
    resid_own = lax.dynamic_slice_in_dim(tokens, offset, width, 1).astype(
        jnp.float32
    ) + sent_and_summed(projected.astype(jnp.bfloat16), "head", 1)
    power = taken_together(jnp.sum(resid_own * resid_own, axis=-1), "head")
    gain_own = lax.dynamic_slice_in_dim(norm_gain, offset, width, 0)
    normed = (resid_own * lax.rsqrt(power[:, None] / model + 1e-05) * gain_own).astype(jnp.bfloat16)
    experts = lax.axis_size("seq") * lax.axis_size("ctx")
    slots = experts * CAP
    chosen = expert_ids[0].reshape(-1)
    onehot = (chosen[:, None] == lax.broadcasted_iota(jnp.int32, (1, experts), 1)).astype(jnp.int32)
    before = jnp.cumsum(onehot, axis=0) - onehot
    target = chosen * CAP + jnp.sum(before * onehot, axis=1)
    matches = target[None, :] == lax.broadcasted_iota(jnp.int32, (slots, 1), 0)
    select = jnp.sum(matches.astype(jnp.float32).reshape(slots, count, -1), axis=-1).astype(
        jnp.bfloat16
    )
    packed = jnp.dot(select, normed, preferred_element_type=jnp.float32).astype(jnp.bfloat16)
    packed = packed.reshape(experts, CAP, normed.shape[1])
    arrived = lax.all_to_all(packed, ("seq", "ctx"), split_axis=0, concat_axis=0, tiled=True)
    rows = arrived.reshape(slots, normed.shape[1])
    piece = lax.all_gather(rows, "head", axis=1, tiled=True)
    gate_rows = gate_weight[0]
    up_rows = up_weight[0]
    gate = jnp.dot(piece, gate_rows, preferred_element_type=jnp.float32)
    up = jnp.dot(piece, up_rows, preferred_element_type=jnp.float32)
    hidden = (gate * jax.nn.sigmoid(1.702 * gate) * (up + 1.0)).astype(jnp.bfloat16)
    columns = down_weight[0]
    expert_out = sent_and_summed(
        jnp.einsum("fd,rf->dr", columns, hidden, preferred_element_type=jnp.float32).astype(
            jnp.bfloat16
        ),
        "head",
        0,
    ).astype(jnp.bfloat16)
    returned = lax.all_to_all(expert_out, ("seq", "ctx"), split_axis=1, concat_axis=1, tiled=True)
    spread_weights = jnp.where(matches.T, expert_weights[0].reshape(-1)[:, None], 0.0)
    spread_weights = jnp.sum(spread_weights.reshape(count, -1, slots), axis=1)
    moe = lax.dot_general(
        spread_weights,
        returned.astype(jnp.float32),
        (((1,), (1,)), ((), ())),
        precision=lax.Precision.HIGHEST,
    )
    return (resid_own + moe).astype(jnp.bfloat16)[None]


def solution(mesh):
    in_specs = (
        P("seq", "ctx", None),
        P(None, "head"),
        P("seq", "ctx", "head", None),
        P("seq", "ctx", "head", None),
        P("seq", "ctx", "head", None),
        P("seq", "ctx", "head", None),
        P("head", None),
        P(),
        P("seq", "ctx", None),
        P("seq", "ctx", None),
        P(("seq", "ctx"), None, "head"),
        P(("seq", "ctx"), None, "head"),
        P(("seq", "ctx"), "head", None),
    )
    out_specs = P("seq", "ctx", "head")
    return jax.shard_map(body, mesh=mesh, in_specs=in_specs, out_specs=out_specs, check_vma=False)
```

profile of v0, /device:TPU:1, one launch (start us, length us, event | category | flops | bytes accessed | tf_op | source)
XLA Modules:
  0.0 326.2 jit_solution(1258331897230026775)
XLA Ops:
  10.4 9.0 %all-to-all-start = ((bf16[8,1,1,512,64]{3,4,2,1,0:T(8,128)(2,1)}), bf16[8,1,1,512,64]{3,4,2,1,0:T(8,128)(2,1)}, u32[]{:S(2)}, u32[]{:S(2)}) async-start(bf16[8,1,1,512,64]{3,4,2,1,0:T(8,128)(2,1)} %broadcast_in_dim.65), calls=%async_computation | async-start | bytes 1048576 | tf_op jit(solution)/shard_map/all_to_all | solution.py:13
  26.4 11.1 %all-to-all-done = bf16[8,1,1,512,64]{3,4,2,1,0:T(8,128)(2,1)} async-done(((bf16[8,1,1,512,64]{3,4,2,1,0:T(8,128)(2,1)}), bf16[8,1,1,512,64]{3,4,2,1,0:T(8,128)(2,1)}, u32[]{:S(2)}, u32[]{:S(2)}) %all-to-all-start) | async-done | bytes 524320 | tf_op jit(solution)/shard_map/all_to_all | solution.py:13
  37.4 55.5 %while.17 = (s32[]{:T(128)}, f32[8,1,512]{2,1,0:T(1,128)S(1)}, f32[8,1,512]{2,1,0:T(1,128)S(1)}, f32[8,1,512,64]{2,3,1,0:T(8,128)}, s32[8]{0:T(128)S(1)}, /*inde...) while((s32[]{:T(128)}, f32[8,1,512]{2,1,0:T(1,128)S(1)}, ...), condition=%wide.region_3.4_spmd.clone, body=%wide.region_0.3_spmd.clone.sunk | while | flops 290915840 | bytes 14024361 | solution.py:109
  46.2 3.0 fusion.82
  53.1 3.0 fusion.82
  60.1 3.0 fusion.82
  67.0 3.0 fusion.82
  73.9 3.0 fusion.82
  80.9 3.0 fusion.82
  92.9 9.0 %all_to_all.53 = f32[8,1,512]{2,1,0:T(1,128)S(1)} all-to-all(f32[8,1,512]{2,1,0:T(1,128)S(1)} %get-tuple-element.143), channel_id=1, replica_groups=mesh['seq'=4,'ctx'=8,'head'=8] {'ctx'}, dimensions={0} | all-to-all | bytes 32768 | tf_op jit(solution)/shard_map/all_to_all | solution.py:110
  102.0 9.0 %all_to_all.54 = f32[8,1,512]{2,1,0:T(1,128)S(1)} all-to-all(f32[8,1,512]{2,1,0:T(1,128)S(1)} %get-tuple-element.144), channel_id=1, replica_groups=mesh['seq'=4,'ctx'=8,'head'=8] {'ctx'}, dimensions={0} | all-to-all | bytes 32768 | tf_op jit(solution)/shard_map/all_to_all | solution.py:110
  110.9 4.2 %all-to-all-start.1 = ((f32[8,1,512,64]{2,3,1,0:T(8,128)}), f32[8,1,512,64]{2,3,1,0:T(8,128)}, u32[]{:S(2)}, u32[]{:S(2)}) async-start(f32[8,1,512,64]{2,3,1,0:T(8,128)} %get-tuple-element.142), calls=%async_computation.1 | async-start | bytes 2097152 | tf_op jit(solution)/shard_map/all_to_all | solution.py:110
  117.8 24.6 %all-to-all-done.1 = f32[8,1,512,64]{2,3,1,0:T(8,128)} async-done(((f32[8,1,512,64]{2,3,1,0:T(8,128)}), f32[8,1,512,64]{2,3,1,0:T(8,128)}, u32[]{:S(2)}, u32[]{:S(2)}) %all-to-all-start.1) | async-done | bytes 1048608 | tf_op jit(solution)/shard_map/all_to_all | solution.py:110
  148.1 5.1 %all-to-all-start.4 = ((bf16[8,64,360]{2,1,0:T(8,128)(2,1)}), bf16[8,64,360]{2,1,0:T(8,128)(2,1)S(1)}, u32[]{:S(2)}, u32[]{:S(2)}) async-start(bf16[8,64,360]{2,1,0:T(8,128)(2,1)} %bitcast.105), calls=%async_computation.4 | async-start | bytes 786432 | tf_op jit(solution)/shard_map/all_to_all | solution.py:34
  153.6 6.3 %all-to-all-done.4 = bf16[8,64,360]{2,1,0:T(8,128)(2,1)S(1)} async-done(((bf16[8,64,360]{2,1,0:T(8,128)(2,1)}), bf16[8,64,360]{2,1,0:T(8,128)(2,1)S(1)}, u32[]{:S(2)}, u32[]{:S(2)}) %all-to-all-start.4) | async-done | bytes 368672 | tf_op jit(solution)/shard_map/all_to_all | solution.py:34
  161.6 3.3 %all-to-all-start.5 = ((f32[8,1,64]{2,1,0:T(1,128)}), f32[8,1,64]{2,1,0:T(1,128)S(1)}, u32[]{:S(2)}, u32[]{:S(2)}) async-start(f32[8,1,64]{2,1,0:T(1,128)} %broadcast_in_dim.69), calls=%async_computation.5 | async-start | bytes 8192 | tf_op jit(solution)/shard_map/all_to_all | solution.py:13
  165.8 3.9 %all-to-all-done.5 = f32[8,1,64]{2,1,0:T(1,128)S(1)} async-done(((f32[8,1,64]{2,1,0:T(1,128)}), f32[8,1,64]{2,1,0:T(1,128)S(1)}, u32[]{:S(2)}, u32[]{:S(2)}) %all-to-all-start.5) | async-done | bytes 2080 | tf_op jit(solution)/shard_map/all_to_all | solution.py:13
  173.0 23.9 %all_to_all.55 = bf16[32,16,360]{2,1,0:T(8,128)(2,1)} all-to-all(bf16[32,16,360]{2,1,0:T(8,128)(2,1)S(1)} %bitcast.126), channel_id=1, replica_groups=mesh['seq'=4,'ctx'=8,'head'=8] {'seq','ctx'}, dimensions={0} | all-to-all | bytes 737280 | tf_op jit(solution)/shard_map/all_to_all | solution.py:144
  198.8 36.6 %all-gather.2.cloned.1.call-done = bf16[512,2880]{0,1:T(8,128)(2,1)} async-done(((bf16[512,360]{0,1:T(8,128)(2,1)}), bf16[512,2880]{0,1:T(8,128)(2,1)}) %all-gather.2.cloned.1.call-update) | async-done | bytes 2949136 | tf_op jit(solution)/shard_map/all_gather | solution.py:146
  235.5 4.7 %fusion.30 = f32[512,360]{0,1:T(8,128)} fusion(bf16[512,2880]{0,1:T(8,128)(2,1)} %all-gather.2.cloned.1.call-done, bf16[1,2880,360]{1,2,0:T(8,128)(2,1)} %param.25), kind=kOutput, calls=%fused_computation.30 | convolution fusion | flops 1061683200 | bytes 5760000 | tf_op jit(solution)/shard_map/dot_general | solution.py:149
  240.1 7.9 %convolution_convert_fusion = bf16[512,2880]{0,1:T(8,128)(2,1)} fusion(bf16[1,360,2880]{2,1,0:T(8,128)(2,1)} %param.27, bf16[512,2880]{0,1:T(8,128)(2,1)} %all-gather.2.cloned.1.call-done, bf16[1,2880,360]{1,2,0:T(8,128)(2,1)} %param.26, f32[512,360]{0,1:T(8,128)} %fusion.30), kind=kOutput, calls=%fused_computation.25 | convolution fusion | flops 2126315520 | bytes 10782720 | tf_op jit(solution)/shard_map/fd,rf->dr/dot_general | solution.py:154
  248.1 37.1 %all_to_all.56 = bf16[8,360,512]{2,1,0:T(8,128)(2,1)} all-to-all(bf16[8,360,512]{2,1,0:T(8,128)(2,1)} %bitcast.121), channel_id=1, replica_groups=mesh['seq'=4,'ctx'=8,'head'=8] {'head'}, dimensions={0} | all-to-all | bytes 5898240 | tf_op jit(solution)/shard_map/all_to_all | solution.py:34
  288.5 14.1 %all-to-all-start.8 = ((bf16[360,32,16]{0,2,1:T(8,128)(2,1)}), bf16[360,32,16]{0,2,1:T(8,128)(2,1)S(1)}, u32[]{:S(2)}, u32[]{:S(2)}) async-start(bf16[360,32,16]{0,2,1:T(8,128)(2,1)} %bitcast.125), calls=%async_computation.8 | async-start | bytes 786432 | tf_op jit(solution)/shard_map/all_to_all | solution.py:160
  303.4 14.1 %all-to-all-done.8 = bf16[360,32,16]{0,2,1:T(8,128)(2,1)S(1)} async-done(((bf16[360,32,16]{0,2,1:T(8,128)(2,1)}), bf16[360,32,16]{0,2,1:T(8,128)(2,1)S(1)}, u32[]{:S(2)}, u32[]{:S(2)}) %all-to-all-start.8) | async-done | bytes 368672 | tf_op jit(solution)/shard_map/all_to_all | solution.py:160
  (112 shorter events, 60.6 us)
Async XLA Ops:
  6.5 137.5 %copy-start = (bf16[512,2880]{0,1:T(8,128)(2,1)S(1)}, bf16[512,2880]{0,1:T(8,128)(2,1)}, u32[]{:S(2)}) copy-start(bf16[512,2880]{0,1:T(8,128)(2,1)} %param.21) | copy-start | bytes 8847364
  6.5 12.8 %copy-start.1 = (bf16[1,2048,1,64]{1,3,2,0:T(8,128)(2,1)S(1)}, bf16[1,2048,1,64]{1,3,2,0:T(8,128)(2,1)}, u32[]{:S(2)}) copy-start(bf16[1,2048,1,64]{1,3,2,0:T(8,128)(2,1)} %param.17) | copy-start | bytes 786436
  6.5 17.6 %copy-start.2 = (bf16[1,64,1,64]{3,1,2,0:T(8,128)(2,1)S(1)}, bf16[1,64,1,64]{3,1,2,0:T(8,128)(2,1)}, u32[]{:S(2)}) copy-start(bf16[1,64,1,64]{3,1,2,0:T(8,128)(2,1)} %param.19) | copy-start | bytes 24580
  6.5 17.6 %copy-start.3 = (bf16[1,64,1,64]{3,1,2,0:T(8,128)(2,1)S(1)}, bf16[1,64,1,64]{3,1,2,0:T(8,128)(2,1)}, u32[]{:S(2)}) copy-start(bf16[1,64,1,64]{3,1,2,0:T(8,128)(2,1)} %param.20) | copy-start | bytes 24580
  10.4 27.1 %all-to-all-start = ((bf16[8,1,1,512,64]{3,4,2,1,0:T(8,128)(2,1)}), bf16[8,1,1,512,64]{3,4,2,1,0:T(8,128)(2,1)}, u32[]{:S(2)}, u32[]{:S(2)}) async-start(bf16[8,1,1,512,64]{3,4,2,1,0:T(8,128)(2,1)} %broadcast_in_dim.65), calls=%async_computation | async-start | bytes 1048576 | tf_op jit(solution)/shard_map/all_to_all | solution.py:13
  37.4 77.7 %copy-start.7 = (s32[1,64,4]{1,2,0:T(4,128)S(1)}, s32[1,64,4]{1,2,0:T(4,128)}, u32[]{:S(2)}) copy-start(s32[1,64,4]{1,2,0:T(4,128)} %param.23) | copy-start | bytes 3076
  110.9 31.5 %all-to-all-start.1 = ((f32[8,1,512,64]{2,3,1,0:T(8,128)}), f32[8,1,512,64]{2,3,1,0:T(8,128)}, u32[]{:S(2)}, u32[]{:S(2)}) async-start(f32[8,1,512,64]{2,3,1,0:T(8,128)} %get-tuple-element.142), calls=%async_computation.1 | async-start | bytes 2097152 | tf_op jit(solution)/shard_map/all_to_all | solution.py:110
  116.9 0.6 copy-start.4
  144.1 9.2 %slice-start = ((s32[32,3]{0,1:T(4,128)}), s32[32,2]{0,1:T(2,128)S(1)}, s32[]{:S(2)}) async-start(s32[32,3]{0,1:T(4,128)} %copy-done.4), calls=%async_computation.10 | async-start | bytes 2048 | tf_op jit(solution)/shard_map/slice.1
  144.1 9.2 %copy-start.5 = (s32[256]{0:T(256)S(1)}, s32[256]{0:T(256)}, u32[]{:S(2)}) copy-start(s32[256]{0:T(256)} %eq.54) | copy-start | bytes 3076
  148.1 11.7 %all-to-all-start.4 = ((bf16[8,64,360]{2,1,0:T(8,128)(2,1)}), bf16[8,64,360]{2,1,0:T(8,128)(2,1)S(1)}, u32[]{:S(2)}, u32[]{:S(2)}) async-start(bf16[8,64,360]{2,1,0:T(8,128)(2,1)} %bitcast.105), calls=%async_computation.4 | async-start | bytes 786432 | tf_op jit(solution)/shard_map/all_to_all | solution.py:34
  161.6 8.2 %all-to-all-start.5 = ((f32[8,1,64]{2,1,0:T(1,128)}), f32[8,1,64]{2,1,0:T(1,128)S(1)}, u32[]{:S(2)}, u32[]{:S(2)}) async-start(f32[8,1,64]{2,1,0:T(1,128)} %broadcast_in_dim.69), calls=%async_computation.5 | async-start | bytes 8192 | tf_op jit(solution)/shard_map/all_to_all | solution.py:13
  164.9 70.6 %all-gather.2.cloned.1.call-start = ((), (), s32[]{:S(2)}) async-start(), calls=%async_computation.9 | async-start | bytes 3317760 | tf_op jit(solution)/shard_map/all_gather | solution.py:146
  285.2 17.4 %copy-start.6 = (f32[1,64,4]{1,2,0:T(4,128)S(1)}, f32[1,64,4]{1,2,0:T(4,128)}, u32[]{:S(2)}) copy-start(f32[1,64,4]{1,2,0:T(4,128)} %param.24) | copy-start | bytes 3076
  288.5 29.0 %all-to-all-start.8 = ((bf16[360,32,16]{0,2,1:T(8,128)(2,1)}), bf16[360,32,16]{0,2,1:T(8,128)(2,1)S(1)}, u32[]{:S(2)}, u32[]{:S(2)}) async-start(bf16[360,32,16]{0,2,1:T(8,128)(2,1)} %bitcast.125), calls=%async_computation.8 | async-start | bytes 786432 | tf_op jit(solution)/shard_map/all_to_all | solution.py:160
Sparse Core Ops, SparseCore 0:
  198.9 36.4 all-gather.1
where the time goes:
time: 328 us; the launch traced here: 326 us
  waiting for transfers between devices  96.7 us (29%)
  blocking collectives  79.1 us (24%)
  matrix products  56.1 us (17%)
  starting transfers between devices  35.8 us (11%)
  local copies, waits for them, and re-layouts  19 us (6%)
  other arithmetic  16 us (5%)
  between operations  13.6 us (4%)
  loops' own time  9.98 us (3%)
    all_to_all x1, blocking collectives, sent_and_summed(): lax.all_to_all(tiles, axis, split_axis=0, concat_axis=0, tiled=True)  37.1 us
    all_gather x1, waiting for transfers between devices, body(): piece = lax.all_gather(rows, 'head', axis=1, tiled=True)  36.6 us
    all_to_all x1, waiting for transfers between devices, body(): lax.all_to_all(pieces, 'ctx', split_axis=0, concat_axis=0, tiled=True)  24.6 us
    dot_general x8, matrix products, absorb(): jnp.einsum('hrd,hkd->hrk', block, keys, preferred_element_type=jnp.float32)  24 us
    all_to_all x1, blocking collectives, body(): lax.all_to_all(packed, ('seq', 'ctx'), split_axis=0, concat_axis=0, tiled...  23.9 us
    all_to_all x2, blocking collectives, body(): lax.all_to_all(pieces, 'ctx', split_axis=0, concat_axis=0, tiled=True)  18 us
    all_to_all x2, waiting for transfers between devices, sent_to_all(): return lax.all_to_all(copies, axis, split_axis=0, concat_axis=0, tiled=True)  15 us
    all_to_all x1, waiting for transfers between devices, body(): lax.all_to_all(expert_out, ('seq', 'ctx'), split_axis=1, concat_axis=1, t...  14.1 us
  transfers between devices with their start and end apart: 6, of which 6 were waited for; matrix products, arithmetic and copies ran while one was open for 3% of the time, Pallas kernels for 0%

commit v1 on v0

--- a/solution.py
+++ b/solution.py
@@ -3,9 +3,287 @@
 import jax
 import jax.numpy as jnp
 from jax import lax
+from jax.experimental import pallas as pl
+from jax.experimental.pallas import tpu as pltpu
 from jax.sharding import PartitionSpec as P
 
 CAP = 16
+MESH = pl.DeviceIdType.MESH
+LOG2E = 1.4426950408889634
+NEG = -3.0e38
+NT = (((1,), (1,)), ((), ()))
+
+
+def remote(src, dst, send, recv, where):
+    return pltpu.make_async_remote_copy(
+        src_ref=src, dst_ref=dst, send_sem=send, recv_sem=recv, device_id=where, device_id_type=MESH
+    )
+
+
+def greet(groups):
+    barrier = pltpu.get_barrier_semaphore()
+    total = 0
+    for axis in groups:
+        size = lax.axis_size(axis)
+        me = lax.axis_index(axis)
+        for step in range(1, size):
+            pl.semaphore_signal(
+                barrier, inc=1, device_id={axis: lax.rem(me + step, size)}, device_id_type=MESH
+            )
+        total += size - 1
+    return barrier, total
+
+
+def attention_kernel(
+    q_ref,
+    kt_ref,
+    vt_ref,
+    nk_ref,
+    nv_ref,
+    own_ref,
+    wo_hbm,
+    resid_ref,
+    qbuf,
+    ke,
+    ko,
+    ve,
+    vo,
+    kn,
+    vn,
+    obuf,
+    lbuf,
+    rbuf,
+    rlse,
+    wo,
+    pbuf,
+    prec,
+    q_send,
+    q_recv,
+    o_send,
+    o_recv,
+    l_send,
+    l_recv,
+    p_send,
+    p_recv,
+    wo_sem,
+):
+    n = lax.axis_size("ctx")
+    place = lax.axis_index("ctx")
+    heads = lax.axis_size("head")
+    lane_of = lax.axis_index("head")
+    barrier, total = greet(("ctx", "head"))
+    wo_copy = pltpu.make_async_copy(wo_hbm, wo, wo_sem)
+    wo_copy.start()
+    rows = q_ref.shape[0]
+    count = nk_ref.shape[0]
+    half = kt_ref.shape[0]
+    cached = kt_ref.shape[1]
+
+    ke[0:half, :] = kt_ref[...]
+    ke[half : 2 * half, :] = jnp.zeros((half, cached), jnp.bfloat16)
+    ko[0:half, :] = jnp.zeros((half, cached), jnp.bfloat16)
+    ko[half : 2 * half, :] = kt_ref[...]
+    qbuf[0] = q_ref[...]
+    low_n = lax.broadcasted_iota(jnp.int32, (count, 2 * half), 1) < half
+    nk = nk_ref[...].astype(jnp.float32)
+    nv = nv_ref[...].astype(jnp.float32)
+    one = jnp.ones((count, 2 * half), jnp.float32)
+    kn[0:count, :] = jnp.where(low_n, nk, 0.0).astype(jnp.bfloat16)
+    kn[count : 2 * count, :] = jnp.where(low_n, 0.0, nk).astype(jnp.bfloat16)
+    vn[0:count, 0 : 2 * half] = jnp.where(low_n, nv, 0.0).astype(jnp.bfloat16)
+    vn[count : 2 * count, 0 : 2 * half] = jnp.where(low_n, 0.0, nv).astype(jnp.bfloat16)
+    vn[0:count, 2 * half : 4 * half] = jnp.where(low_n, one, 0.0).astype(jnp.bfloat16)
+    vn[count : 2 * count, 2 * half : 4 * half] = jnp.where(low_n, 0.0, one).astype(jnp.bfloat16)
+
+    pl.semaphore_wait(barrier, total)
+    right = lax.rem(place + 1, n)
+    left = lax.rem(place + n - 1, n)
+    remote(q_ref, qbuf.at[1], q_send.at[1], q_recv.at[1], {"ctx": right}).start()
+    remote(q_ref, qbuf.at[2], q_send.at[2], q_recv.at[2], {"ctx": left}).start()
+
+    wide = 256
+
+    @pl.loop(0, cached // wide)
+    def _(c):
+        at = pl.ds(pl.multiple_of(c * wide, wide), wide)
+        low = lax.broadcasted_iota(jnp.int32, (wide, 2 * half), 1) < half
+        ones = jnp.where(low, 1.0, 0.0)
+        v = vt_ref[:, at].astype(jnp.float32)
+        blank = jnp.zeros_like(v)
+        ve[at, 0 : 2 * half] = jnp.concatenate([v, blank], 0).T.astype(jnp.bfloat16)
+        vo[at, 0 : 2 * half] = jnp.concatenate([blank, v], 0).T.astype(jnp.bfloat16)
+        ve[at, 2 * half : 4 * half] = ones.astype(jnp.bfloat16)
+        vo[at, 2 * half : 4 * half] = (1.0 - ones).astype(jnp.bfloat16)
+
+    lane = lax.broadcasted_iota(jnp.int32, (rows, 2 * half), 1)
+    low = lane < half
+    tok = lax.rem(lax.broadcasted_iota(jnp.int32, (rows, 2 * half), 0), count)
+    pos = lax.rem(lane, half)
+
+    def offset_of(k):
+        return lax.div(k + 1, 2) * (1 - 2 * lax.rem(k, 2))
+
+    @pl.loop(0, n)
+    def _(k):
+        @pl.when(k > 0)
+        def _():
+            remote(
+                qbuf.at[k], qbuf.at[k], q_send.at[k], q_recv.at[k], {"ctx": right}
+            ).wait_recv()
+
+            @pl.when(k + 2 < n)
+            def _():
+                onward = lax.rem(place + n + 1 - 2 * lax.rem(k + 1, 2), n)
+                remote(
+                    qbuf.at[k],
+                    qbuf.at[k + 2],
+                    q_send.at[k + 2],
+                    q_recv.at[k + 2],
+                    {"ctx": onward},
+                ).start()
+
+        source = lax.rem(place + offset_of(k) + n, n)
+        q = qbuf[k]
+        s_e = jnp.dot(q, ke[...], preferred_element_type=jnp.float32)
+        s_o = jnp.dot(q, ko[...], preferred_element_type=jnp.float32)
+        s_n = lax.dot_general(q, kn[...], NT, preferred_element_type=jnp.float32)
+        ahead = jnp.where(place < source, count, jnp.where(place == source, 0, -count - 1))
+        s_n = jnp.where(pos <= tok + ahead, s_n, NEG)
+        m_e = jnp.maximum(
+            jnp.max(s_e, axis=1, keepdims=True),
+            jnp.max(jnp.where(low, s_n, NEG), axis=1, keepdims=True),
+        )
+        m_o = jnp.maximum(
+            jnp.max(s_o, axis=1, keepdims=True),
+            jnp.max(jnp.where(low, NEG, s_n), axis=1, keepdims=True),
+        )
+        p_e = jnp.exp2((s_e - m_e) * LOG2E).astype(jnp.bfloat16)
+        p_o = jnp.exp2((s_o - m_o) * LOG2E).astype(jnp.bfloat16)
+        tops = jnp.where(low, m_e, m_o)
+        p_n = jnp.exp2((s_n - tops) * LOG2E).astype(jnp.bfloat16)
+        acc = (
+            jnp.dot(p_e, ve[...], preferred_element_type=jnp.float32)
+            + jnp.dot(p_o, vo[...], preferred_element_type=jnp.float32)
+            + jnp.dot(p_n, vn[...], preferred_element_type=jnp.float32)
+        )
+        num = acc[:, 0 : 2 * half]
+        tot = acc[:, 2 * half : 4 * half]
+        obuf[k] = (num / tot).astype(jnp.bfloat16)
+        turned = (tops + jnp.log(tot)).T
+        first = lax.broadcasted_iota(jnp.int32, (8, rows), 0) < 4
+        lbuf[k] = jnp.where(first, turned[0:8, :], turned[half : half + 8, :])
+
+        @pl.when(k > 0)
+        def _():
+            there = {"ctx": source}
+            remote(obuf.at[k], rbuf.at[k], o_send.at[k], o_recv.at[k], there).start()
+            remote(lbuf.at[k], rlse.at[k], l_send.at[k], l_recv.at[k], there).start()
+
+    @pl.loop(1, n)
+    def _(k):
+        here = {"ctx": right}
+        remote(obuf.at[k], rbuf.at[k], o_send.at[k], o_recv.at[k], here).wait_recv()
+        remote(lbuf.at[k], rlse.at[k], l_send.at[k], l_recv.at[k], here).wait_recv()
+
+    rbuf[0] = obuf[0]
+    rlse[0] = lbuf[0]
+    lse = [rlse[k] for k in range(n)]
+    peak = lse[0]
+    for k in range(1, n):
+        peak = jnp.maximum(peak, lse[k])
+    parts = [jnp.exp(x - peak) for x in lse]
+    whole = parts[0]
+    for k in range(1, n):
+        whole = whole + parts[k]
+    share = jnp.concatenate([x / whole for x in parts], axis=0)
+    share = jnp.concatenate([share, share], axis=0).T
+    upper = share.astype(jnp.bfloat16).astype(jnp.float32)
+    first = lax.broadcasted_iota(jnp.int32, share.shape, 1) < 8 * n
+    split = jnp.where(first, upper, share - upper).astype(jnp.bfloat16)
+    col = lax.broadcasted_iota(jnp.int32, (16 * n, 2 * half * n), 1)
+    row = lax.broadcasted_iota(jnp.int32, (16 * n, 2 * half * n), 0)
+    wanted = lax.div(col, 2 * half) * 8 + jnp.where(lax.rem(col, 2 * half) < half, 0, 4)
+    pick = jnp.where(lax.rem(row, 8 * n) == wanted, 1.0, 0.0).astype(jnp.bfloat16)
+    factor = jnp.dot(split, pick, preferred_element_type=jnp.float32)
+    attn = jnp.zeros((rows, 2 * half), jnp.float32)
+    for k in range(n):
+        attn = attn + factor[:, 2 * half * k : 2 * half * (k + 1)] * rbuf[k].astype(jnp.float32)
+    attn = attn.astype(jnp.bfloat16)
+    flat = jnp.concatenate([attn[count * j : count * (j + 1), :] for j in range(rows // count)], axis=1)
+
+    wo_copy.wait()
+
+    @pl.loop(0, heads - 1)
+    def _(c):
+        there = lax.rem(lane_of + 1 + c, heads)
+        part = lax.dot_general(flat, wo[there], NT, preferred_element_type=jnp.float32)
+        pbuf[c] = part.astype(jnp.bfloat16)
+        remote(pbuf.at[c], prec.at[c], p_send.at[c], p_recv.at[c], {"head": there}).start()
+
+    mine = lax.dot_general(flat, wo[lane_of], NT, preferred_element_type=jnp.float32)
+    acc = own_ref[...] + mine
+    for c in range(heads - 1):
+        there = lax.rem(lane_of + 1 + c, heads)
+        remote(pbuf.at[c], prec.at[c], p_send.at[c], p_recv.at[c], {"head": there}).wait_recv()
+        acc = acc + prec[c].astype(jnp.float32)
+    resid_ref[...] = acc
+
+    @pl.loop(1, n)
+    def _(k):
+        here = {"ctx": right}
+        remote(qbuf.at[k], qbuf.at[k], q_send.at[k], q_recv.at[k], here).wait_send()
+        remote(obuf.at[k], rbuf.at[k], o_send.at[k], o_recv.at[k], here).wait_send()
+        remote(lbuf.at[k], rlse.at[k], l_send.at[k], l_recv.at[k], here).wait_send()
+
+    @pl.loop(0, heads - 1)
+    def _(c):
+        there = lax.rem(lane_of + 1 + c, heads)
+        remote(pbuf.at[c], prec.at[c], p_send.at[c], p_recv.at[c], {"head": there}).wait_send()
+
+
+def attend(q, kt, vt, nk, nv, own, wo):
+    n = lax.axis_size("ctx")
+    rows, wide = q.shape
+    cached = kt.shape[1]
+    count, width = own.shape
+    heads = wo.shape[0]
+    bf = jnp.bfloat16
+    vm = pl.BlockSpec(memory_space=pltpu.VMEM)
+    dma = pltpu.SemaphoreType.DMA
+    return pl.pallas_call(
+        attention_kernel,
+        out_shape=jax.ShapeDtypeStruct((count, width), jnp.float32),
+        in_specs=[vm] * 6 + [pl.BlockSpec(memory_space=pl.ANY)],
+        out_specs=vm,
+        scratch_shapes=[
+            pltpu.VMEM((n, rows, wide), bf),
+            pltpu.VMEM((wide, cached), bf),
+            pltpu.VMEM((wide, cached), bf),
+            pltpu.VMEM((cached, 2 * wide), bf),
+            pltpu.VMEM((cached, 2 * wide), bf),
+            pltpu.VMEM((2 * count, wide), bf),
+            pltpu.VMEM((2 * count, 2 * wide), bf),
+            pltpu.VMEM((n, rows, wide), bf),
+            pltpu.VMEM((n, 8, rows), jnp.float32),
+            pltpu.VMEM((n, rows, wide), bf),
+            pltpu.VMEM((n, 8, rows), jnp.float32),
+            pltpu.VMEM(wo.shape, bf),
+            pltpu.VMEM((heads - 1, count, width), bf),
+            pltpu.VMEM((heads - 1, count, width), bf),
+            dma((n,)),
+            dma((n,)),
+            dma((n,)),
+            dma((n,)),
+            dma((n,)),
+            dma((n,)),
+            dma((heads - 1,)),
+            dma((heads - 1,)),
+            dma,
+        ],
+        compiler_params=pltpu.CompilerParams(
+            collective_id=0, has_side_effects=True, vmem_limit_bytes=40 * 1024 * 1024
+        ),
+    )(q, kt, vt, nk, nv, own, wo)
 
 
 def sent_to_all(array, axis):
@@ -60,72 +338,26 @@
     kv_local = cache_keys.shape[2]
     head_dim = cache_keys.shape[3]
     group = query_weight.shape[1] // (kv_local * head_dim)
-    cache_len = cache_keys.shape[1]
-    height = count * group
-    cycles = lax.axis_size("ctx")
-    place = lax.axis_index("ctx")
     scale = 1.0 / math.sqrt(head_dim)
+    heads = lax.axis_size("head")
+    width = model // heads
+    offset = lax.axis_index("head") * width
     query = jnp.dot(tokens, query_weight, preferred_element_type=jnp.float32).astype(jnp.bfloat16)
-    query = (
-        query.reshape(count, kv_local, group, head_dim)
-        .transpose(1, 0, 2, 3)
-        .reshape(kv_local, height, head_dim)
+    query = query * jnp.bfloat16(scale)
+    pairs = group * head_dim // 128
+    query = query.reshape(count, pairs, 128).transpose(1, 0, 2).reshape(pairs * count, 128)
+    fresh_keys = new_keys[0, :, 0, :]
+    fresh_values = new_values[0, :, 0, :]
+    own = lax.dynamic_slice_in_dim(tokens, offset, width, 1).astype(jnp.float32)
+    resid_own = attend(
+        query,
+        cache_keys[0, :, 0, :].T,
+        cache_values[0, :, 0, :].T,
+        jnp.concatenate([fresh_keys, fresh_keys], axis=1),
+        jnp.concatenate([fresh_values, fresh_values], axis=1),
+        own,
+        out_weight.T.reshape(heads, width, out_weight.shape[0]),
     )
-    keys = jnp.concatenate([cache_keys[0], new_keys[0]], axis=0).transpose(1, 0, 2)
-    values = jnp.concatenate([cache_values[0], new_values[0]], axis=0).transpose(1, 0, 2)
-    extent = keys.shape[1]
-    key_index = lax.broadcasted_iota(jnp.int32, (height, extent), 1)
-    tok_index = lax.broadcasted_iota(jnp.int32, (height, extent), 0) // group
-    fresh = key_index - cache_len
-    blank = (
-        jnp.full((kv_local, height), -jnp.inf, jnp.float32),
-        jnp.zeros((kv_local, height), jnp.float32),
-        jnp.zeros((kv_local, height, head_dim), jnp.float32),
-    )
-
-    def absorb(block, state, sources):
-        top, total, numerator = state
-        anchor = sources[:, None]
-        allowed = (
-            (key_index < cache_len) | (place < anchor) | (place == anchor) & (fresh <= tok_index)
-        )
-        scores = jnp.einsum("hrd,hkd->hrk", block, keys, preferred_element_type=jnp.float32) * scale
-        scores = jnp.where(allowed[None], scores, -jnp.inf)
-        new_top = jnp.max(scores, axis=-1)
-        weights = jnp.exp(scores - new_top[..., None])
-        fade = jnp.exp(top - new_top)
-        total = total * fade + jnp.sum(weights, axis=-1)
-        numerator = numerator * fade[..., None] + jnp.einsum(
-            "hrk,hkd->hrd", weights.astype(jnp.bfloat16), values, preferred_element_type=jnp.float32
-        )
-        return (new_top, total, numerator)
-
-    everyone = gathered_copies(query[None], "ctx", 0)
-
-    def partial_state(operands):
-        block, source = operands
-        return absorb(block, blank, jnp.full((height,), source, jnp.int32))
-
-    pieces = lax.map(partial_state, (everyone, lax.iota(jnp.int32, cycles)))
-    tops, totals, numerators = lax.all_to_all(
-        pieces, "ctx", split_axis=0, concat_axis=0, tiled=True
-    )
-    top = jnp.max(tops, axis=0)
-    fade = jnp.exp(tops - top[None])
-    total = jnp.sum(totals * fade, axis=0)
-    numerator = jnp.sum(numerators * fade[..., None], axis=0)
-    attn = (numerator / total[..., None]).astype(jnp.bfloat16)
-    attn = (
-        attn.reshape(kv_local, count, group, head_dim)
-        .transpose(1, 0, 2, 3)
-        .reshape(count, kv_local * group * head_dim)
-    )
-    projected = jnp.dot(attn, out_weight, preferred_element_type=jnp.float32)
-    width = model // lax.axis_size("head")
-    offset = lax.axis_index("head") * width
-    resid_own = lax.dynamic_slice_in_dim(tokens, offset, width, 1).astype(
-        jnp.float32
-    ) + sent_and_summed(projected.astype(jnp.bfloat16), "head", 1)
     power = taken_together(jnp.sum(resid_own * resid_own, axis=-1), "head")
     gain_own = lax.dynamic_slice_in_dim(norm_gain, offset, width, 0)
     normed = (resid_own * lax.rsqrt(power[:, None] / model + 1e-05) * gain_own).astype(jnp.bfloat16)

time: 328 us -> 223 us (0.68)
  Pallas kernels: 0 us -> 46.4 us
  waiting for transfers between devices: 96.7 us -> 53.3 us
  matrix products: 56.1 us -> 17.3 us
  starting transfers between devices: 35.8 us -> 17.4 us
  blocking collectives: 79.1 us -> 62.1 us
  local copies, waits for them, and re-layouts: 19 us -> 6.88 us
  other arithmetic: 16 us -> 5.37 us
  loops' own time: 9.98 us -> 0 us
    pallas_call x0 -> x1, Pallas kernels: none -> 46.4 us  [attend(): pl.pallas_call(attention_kernel, out_shape=jax.ShapeDtypeStruct((count, w...]
    dot_general x17 -> x0, matrix products: 36.9 us -> none  [the longest x8 24 us: absorb(): jnp.einsum('hrd,hkd->hrk', block, keys, preferred_element_type=jnp.float32)]
    all_to_all x2 -> x0, waiting for transfers between devices: 30.9 us -> none  [the longest x1 24.6 us: body(): lax.all_to_all(pieces, 'ctx', split_axis=0, concat_axis=0, tiled=True)]
    all_to_all x2 -> x0, blocking collectives: 18 us -> none  [body(): lax.all_to_all(pieces, 'ctx', split_axis=0, concat_axis=0, tiled=True)]
    all_to_all x2 -> x1, waiting for transfers between devices: 15 us -> 2.52 us  [sent_to_all(): return lax.all_to_all(copies, axis, split_axis=0, concat_axis=0, tiled=True)]
    another operation x1 -> x0, loops' own time: 9.98 us -> none  [body(): pieces = lax.map(partial_state, (everyone, lax.iota(jnp.int32, cycles)))]
    all_to_all x2 -> x0, starting transfers between devices: 9.36 us -> none  [the longest x1 5.12 us: sent_and_summed(): lax.all_to_all(tiles, axis, split_axis=0, concat_axis=0, tiled=True)]
    all_to_all x2 -> x1, starting transfers between devices: 12.3 us -> 3.31 us  [sent_to_all(): return lax.all_to_all(copies, axis, split_axis=0, concat_axis=0, tiled=True)]
  transfers between devices with their start and end apart: 6 -> 3, of which waited for: 6 -> 3; matrix products, arithmetic and copies ran while one was open for 3% -> 1% of each run, Pallas kernels for 0% -> 0%
where the time goes in v1:
time: 223 us; the launch traced here: 222 us
  blocking collectives  62.1 us (28%)
  waiting for transfers between devices  53.3 us (24%)
  Pallas kernels  46.4 us (21%)
  starting transfers between devices  17.4 us (8%)
  matrix products  17.3 us (8%)
  between operations  13.6 us (6%)
  local copies, waits for them, and re-layouts  6.88 us (3%)
  other arithmetic  5.37 us (2%)
    pallas_call x1, Pallas kernels, attend(): pl.pallas_call(attention_kernel, out_shape=jax.ShapeDtypeStruct((count, w...  46.4 us
    all_to_all x1, blocking collectives, sent_and_summed(): lax.all_to_all(tiles, axis, split_axis=0, concat_axis=0, tiled=True)  37.1 us
    all_gather x1, waiting for transfers between devices, body(): piece = lax.all_gather(rows, 'head', axis=1, tiled=True)  36.6 us
    all_to_all x1, blocking collectives, body(): lax.all_to_all(packed, ('seq', 'ctx'), split_axis=0, concat_axis=0, tiled...  25 us
    all_to_all x1, waiting for transfers between devices, body(): lax.all_to_all(expert_out, ('seq', 'ctx'), split_axis=1, concat_axis=1, t...  14.1 us
    all_to_all x1, starting transfers between devices, body(): lax.all_to_all(expert_out, ('seq', 'ctx'), split_axis=1, concat_axis=1, t...  14.1 us
    dot_general x1, matrix products, body(): jnp.einsum('fd,rf->dr', columns, hidden, preferred_element_type=jnp.float32)  7.94 us
    dot_general x1, matrix products, body(): gate = jnp.dot(piece, gate_rows, preferred_element_type=jnp.float32)  4.67 us
  transfers between devices with their start and end apart: 3, of which 3 were waited for; matrix products, arithmetic and copies ran while one was open for 1% of the time, Pallas kernels for 0%

profile of v1, /device:TPU:1, one launch (start us, length us, event | category | flops | bytes accessed | tf_op | source)
XLA Modules:
  0.0 222.3 jit_solution(4476405195241113505)
XLA Ops:
  6.6 1.1 bitcast_convert_fusion.own_ref
  7.6 0.8 copy-done
  8.4 1.7 fusion.16
  10.3 46.4 %shard_map.127 = f32[64,360]{1,0:T(8,128)S(1)} custom-call(bf16[256,128]{1,0:T(8,128)(2,1)S(1)} %bitcast.83, bf16[64,2048]{1,0:T(8,128)(2,1)S(1)} %bitcast.81, bf16[64,2048]{1,0:T(8,128)(2,1)S(1)} %bitcast.82, bf16[64,128]{1,0:T(8,128)(2,1)S(1)} %get-tuple-element.5.nk_ref, bf16[64,128]{1,0:T(8,128)(2,1)S(1)} %get-tuple-element.6.nv_ref, ...), custom_call_target="tpu_custom_call" | custom-call | tf_op jit(solution)/shard_map/pallas_call | solution.py:253
  56.8 0.6 broadcast_in_dim.26
  57.4 3.3 %all-to-all-start = ((f32[8,1,64]{2,1,0:T(1,128)}), f32[8,1,64]{2,1,0:T(1,128)S(1)}, u32[]{:S(2)}, u32[]{:S(2)}) async-start(f32[8,1,64]{2,1,0:T(1,128)} %broadcast_in_dim.26), calls=%async_computation | async-start | bytes 8192 | tf_op jit(solution)/shard_map/all_to_all | solution.py:291
  61.1 0.6 reduce-window.6
  61.7 0.2 slice_reduce_fusion
  62.4 0.8 dynamic_slice.7
  63.1 2.5 %all-to-all-done = f32[8,1,64]{2,1,0:T(1,128)S(1)} async-done(((f32[8,1,64]{2,1,0:T(1,128)}), f32[8,1,64]{2,1,0:T(1,128)S(1)}, u32[]{:S(2)}, u32[]{:S(2)}) %all-to-all-start) | async-done | bytes 2080 | tf_op jit(solution)/shard_map/all_to_all | solution.py:291
  65.7 1.1 convolution_convert_fusion.1
  66.8 1.2 copy.52
  68.0 25.0 %all_to_all.28 = bf16[32,16,360]{2,1,0:T(8,128)(2,1)} all-to-all(bf16[32,16,360]{2,1,0:T(8,128)(2,1)S(1)} %bitcast.85), channel_id=1, replica_groups=mesh['seq'=4,'ctx'=8,'head'=8] {'seq','ctx'}, dimensions={0} | all-to-all | bytes 737280 | tf_op jit(solution)/shard_map/all_to_all | solution.py:376
  93.0 1.9 copy.53
  94.9 36.6 %all-gather.2.cloned.1.call-done = bf16[512,2880]{0,1:T(8,128)(2,1)} async-done(((bf16[512,360]{0,1:T(8,128)(2,1)}), bf16[512,2880]{0,1:T(8,128)(2,1)}) %all-gather.2.cloned.1.call-update) | async-done | bytes 2949136 | tf_op jit(solution)/shard_map/all_gather | solution.py:378
  131.6 4.7 %fusion.3 = f32[512,360]{0,1:T(8,128)} fusion(bf16[512,2880]{0,1:T(8,128)(2,1)} %all-gather.2.cloned.1.call-done, bf16[1,2880,360]{1,2,0:T(8,128)(2,1)} %param.23), kind=kOutput, calls=%fused_computation.4 | convolution fusion | flops 1061683200 | bytes 5760000 | tf_op jit(solution)/shard_map/dot_general | solution.py:381
  136.3 7.9 %convolution_convert_fusion = bf16[512,2880]{0,1:T(8,128)(2,1)} fusion(bf16[1,360,2880]{2,1,0:T(8,128)(2,1)} %param.25, bf16[512,2880]{0,1:T(8,128)(2,1)} %all-gather.2.cloned.1.call-done, bf16[1,2880,360]{1,2,0:T(8,128)(2,1)} %param.24, f32[512,360]{0,1:T(8,128)} %fusion.3), kind=kOutput, calls=%fused_computation | convolution fusion | flops 2126315520 | bytes 10782720 | tf_op jit(solution)/shard_map/fd,rf->dr/dot_general | solution.py:386
  144.2 37.1 %all_to_all.29 = bf16[8,360,512]{2,1,0:T(8,128)(2,1)} all-to-all(bf16[8,360,512]{2,1,0:T(8,128)(2,1)} %bitcast.84), channel_id=1, replica_groups=mesh['seq'=4,'ctx'=8,'head'=8] {'head'}, dimensions={0} | all-to-all | bytes 5898240 | tf_op jit(solution)/shard_map/all_to_all | solution.py:312
  181.3 2.4 %reduce_sum.65 = bf16[360,512]{1,0:T(8,128)(2,1)S(1)} reduce(bf16[8,360,512]{2,1,0:T(8,128)(2,1)} %all_to_all.29, bf16[]{:T(256)} %constant.31.clone.1), dimensions={0}, to_apply=%region_7.8 | reduce | flops 1290240 | bytes 3317762 | tf_op jit(solution)/shard_map/reduce_sum | solution.py:313
  183.7 0.9 copy.54
  184.7 14.1 %all-to-all-start.3 = ((bf16[360,32,16]{0,2,1:T(8,128)(2,1)}), bf16[360,32,16]{0,2,1:T(8,128)(2,1)S(1)}, u32[]{:S(2)}, u32[]{:S(2)}) async-start(bf16[360,32,16]{0,2,1:T(8,128)(2,1)} %bitcast.23), calls=%async_computation.3 | async-start | bytes 786432 | tf_op jit(solution)/shard_map/all_to_all | solution.py:392
  198.7 0.8 select_reduce_fusion
  199.5 14.1 %all-to-all-done.3 = bf16[360,32,16]{0,2,1:T(8,128)(2,1)S(1)} async-done(((bf16[360,32,16]{0,2,1:T(8,128)(2,1)}), bf16[360,32,16]{0,2,1:T(8,128)(2,1)S(1)}, u32[]{:S(2)}, u32[]{:S(2)}) %all-to-all-start.3) | async-done | bytes 368672 | tf_op jit(solution)/shard_map/all_to_all | solution.py:392
  213.6 1.8 fusion.17
  (33 shorter events, 1.1 us)
Async XLA Ops:
  6.5 1.9 copy-start
  6.5 3.6 %copy-start.4 = (bf16[1,64,1,64]{3,1,2,0:T(8,128)(2,1)S(1)}, bf16[1,64,1,64]{3,1,2,0:T(8,128)(2,1)}, u32[]{:S(2)}) copy-start(bf16[1,64,1,64]{3,1,2,0:T(8,128)(2,1)} %param.17) | copy-start | bytes 24580
  6.5 3.6 %copy-start.5 = (bf16[1,64,1,64]{3,1,2,0:T(8,128)(2,1)S(1)}, bf16[1,64,1,64]{3,1,2,0:T(8,128)(2,1)}, u32[]{:S(2)}) copy-start(bf16[1,64,1,64]{3,1,2,0:T(8,128)(2,1)} %param.18) | copy-start | bytes 24580
  6.5 3.7 %copy-start.2 = (bf16[1,2048,1,64]{1,3,2,0:T(8,128)(2,1)S(1)}, bf16[1,2048,1,64]{1,3,2,0:T(8,128)(2,1)}, u32[]{:S(2)}) copy-start(bf16[1,2048,1,64]{1,3,2,0:T(8,128)(2,1)} %param.15) | copy-start | bytes 786436
  6.5 3.7 %copy-start.1 = (bf16[512,2880]{0,1:T(8,128)(2,1)S(1)}, bf16[512,2880]{0,1:T(8,128)(2,1)}, u32[]{:S(2)}) copy-start(bf16[512,2880]{0,1:T(8,128)(2,1)} %param.19) | copy-start | bytes 8847364
  6.5 3.7 %copy-start.3 = (bf16[1,2048,1,64]{1,3,2,0:T(8,128)(2,1)S(1)}, bf16[1,2048,1,64]{1,3,2,0:T(8,128)(2,1)}, u32[]{:S(2)}) copy-start(bf16[1,2048,1,64]{1,3,2,0:T(8,128)(2,1)} %param.16) | copy-start | bytes 786436
  8.4 52.4 %copy-start.7 = (s32[1,64,4]{1,2,0:T(4,128)S(1)}, s32[1,64,4]{1,2,0:T(4,128)}, u32[]{:S(2)}) copy-start(s32[1,64,4]{1,2,0:T(4,128)} %param.21) | copy-start | bytes 3076
  57.4 8.3 %all-to-all-start = ((f32[8,1,64]{2,1,0:T(1,128)}), f32[8,1,64]{2,1,0:T(1,128)S(1)}, u32[]{:S(2)}, u32[]{:S(2)}) async-start(f32[8,1,64]{2,1,0:T(1,128)} %broadcast_in_dim.26), calls=%async_computation | async-start | bytes 8192 | tf_op jit(solution)/shard_map/all_to_all | solution.py:291
  60.7 70.9 %all-gather.2.cloned.1.call-start = ((), (), s32[]{:S(2)}) async-start(), calls=%async_computation.4 | async-start | bytes 3317760 | tf_op jit(solution)/shard_map/all_gather | solution.py:378
  181.3 17.4 %copy-start.6 = (f32[1,64,4]{1,2,0:T(4,128)S(1)}, f32[1,64,4]{1,2,0:T(4,128)}, u32[]{:S(2)}) copy-start(f32[1,64,4]{1,2,0:T(4,128)} %param.22) | copy-start | bytes 3076
  184.7 29.0 %all-to-all-start.3 = ((bf16[360,32,16]{0,2,1:T(8,128)(2,1)}), bf16[360,32,16]{0,2,1:T(8,128)(2,1)S(1)}, u32[]{:S(2)}, u32[]{:S(2)}) async-start(bf16[360,32,16]{0,2,1:T(8,128)(2,1)} %bitcast.23), calls=%async_computation.3 | async-start | bytes 786432 | tf_op jit(solution)/shard_map/all_to_all | solution.py:392
Sparse Core Ops, SparseCore 0:
  95.1 36.4 all-gather.1

commit v2 on v1

--- a/solution.py
+++ b/solution.py
@@ -286,35 +286,391 @@
     )(q, kt, vt, nk, nv, own, wo)
 
 
-def sent_to_all(array, axis):
-    copies = jnp.broadcast_to(array, (lax.axis_size(axis), *array.shape))
-    return lax.all_to_all(copies, axis, split_axis=0, concat_axis=0, tiled=True)
-
-
-def joined_along(tiles, dim):
-    shape = list(tiles.shape[1:])
-    shape[dim] *= tiles.shape[0]
-    return jnp.moveaxis(tiles, 0, dim).reshape(shape)
-
-
-def gathered_copies(array, axis, dim):
-    tiles = sent_to_all(array, axis)
-    return joined_along(tiles, dim)
-
-
-def split_up(array, dim, count):
-    before, after = (array.shape[:dim], array.shape[dim + 1 :])
-    return jnp.moveaxis(array.reshape(*before, count, -1, *after), dim, 0)
-
-
-def sent_and_summed(array, axis, dim):
-    tiles = split_up(array, dim, lax.axis_size(axis))
-    arrived = lax.all_to_all(tiles, axis, split_axis=0, concat_axis=0, tiled=True)
-    return arrived.astype(jnp.float32).sum(axis=0)
-
-
-def taken_together(array, axis):
-    return sent_to_all(array, axis).sum(axis=0)
+GROUPS = 4
+
+
+def expert_kernel(
+    resid_ref,
+    gain_ref,
+    ids_ref,
+    weights_ref,
+    gate_hbm,
+    up_hbm,
+    down_hbm,
+    out_ref,
+    raw,
+    wide,
+    wgu,
+    wdn,
+    packed,
+    xall,
+    acc,
+    hidden,
+    sbuf,
+    rbuf,
+    final,
+    back,
+    w_sem,
+    d_send,
+    d_recv,
+    g_send,
+    g_recv,
+    s_send,
+    s_recv,
+    b_send,
+    b_recv,
+):
+    seqs, ctxs, heads = lax.axis_size("seq"), lax.axis_size("ctx"), lax.axis_size("head")
+    s, c, h = lax.axis_index("seq"), lax.axis_index("ctx"), lax.axis_index("head")
+    experts = seqs * ctxs
+    count, width = resid_ref.shape
+    padded = wide.shape[1]
+    block = ctxs * CAP
+    f32, bf = jnp.float32, jnp.bfloat16
+    ring = heads // 2
+    col, y = lax.div(h, ring), lax.rem(h, ring)
+
+    def head_at(across, dy):
+        return (col if across == 0 else 1 - col) * ring + lax.rem(y + dy + ring, ring)
+
+    other, above, below = head_at(1, 0), head_at(0, 1), head_at(0, -1)
+    barrier = pltpu.get_barrier_semaphore()
+
+    @pl.loop(1, experts)
+    def _(step):
+        there = {
+            "seq": lax.rem(s + lax.div(step, ctxs), seqs),
+            "ctx": lax.rem(c + lax.rem(step, ctxs), ctxs),
+        }
+        pl.semaphore_signal(barrier, inc=1, device_id=there, device_id_type=MESH)
+
+    for peer in (other, above, below):
+        pl.semaphore_signal(barrier, inc=1, device_id={"head": peer}, device_id_type=MESH)
+    loads = [
+        pltpu.make_async_copy(source, raw.at[i], w_sem.at[i])
+        for i, source in enumerate((gate_hbm, up_hbm, down_hbm))
+    ]
+    for load in loads:
+        load.start()
+
+    ids = ids_ref[...]
+    given = weights_ref[...]
+    index = lax.broadcasted_iota(jnp.int32, (count, experts), 1)
+    named = jnp.zeros((count, experts), f32)
+    amount = jnp.zeros((count, experts), f32)
+    for j in range(ids.shape[1]):
+        hit = ids[:, j : j + 1] == index
+        named = named + jnp.where(hit, 1.0, 0.0)
+        amount = amount + jnp.where(hit, given[:, j : j + 1], 0.0)
+    before = jnp.where(
+        lax.broadcasted_iota(jnp.int32, (count, count), 1)
+        < lax.broadcasted_iota(jnp.int32, (count, count), 0),
+        1.0,
+        0.0,
+    ).astype(bf)
+    rank = jnp.dot(before, named.astype(bf), preferred_element_type=f32)
+    key = jnp.where(named > 0.5, rank, 128.0)
+    spread = jnp.where(
+        lax.div(lax.broadcasted_iota(jnp.int32, (experts, experts * CAP), 1), CAP)
+        == lax.broadcasted_iota(jnp.int32, (experts, experts * CAP), 0),
+        1.0,
+        0.0,
+    ).astype(bf)
+    key = jnp.dot(key.astype(bf), spread, preferred_element_type=f32)
+    slot = lax.rem(lax.broadcasted_iota(jnp.int32, (count, experts * CAP), 1), CAP).astype(f32)
+    chosen = key == slot
+    select = jnp.where(chosen, 1.0, 0.0).T.astype(bf)
+
+    def pieces(x):
+        one = x.astype(bf)
+        rest = x - one.astype(f32)
+        two = rest.astype(bf)
+        return one, two, (rest - two.astype(f32)).astype(bf)
+
+    factors = []
+    for piece in pieces(amount):
+        on_slots = jnp.dot(piece, spread, preferred_element_type=f32)
+        factors.append(jnp.where(chosen, on_slots, 0.0).astype(bf))
+
+    resid = resid_ref[...]
+    wide[...] = jnp.zeros(wide.shape, f32)
+    wide[:, 0:width] = resid * gain_ref[...]
+    power = jnp.sum(resid * resid, axis=1, keepdims=True)
+    lane = lax.broadcasted_iota(jnp.int32, (count, padded), 1)
+    row = wide[...]
+    for i, piece in enumerate(pieces(power)):
+        row = jnp.where(lane == width + i, piece.astype(f32), row)
+    packed[...] = jnp.dot(select, row.astype(bf), preferred_element_type=f32).astype(bf)
+
+    me = s * ctxs + c
+    mine = pl.ds(pl.multiple_of(me * CAP, CAP), CAP)
+    pl.semaphore_wait(barrier, experts - 1 + 3)
+
+    @pl.loop(1, experts)
+    def _(step):
+        s_to = lax.rem(s + seqs - lax.div(step, ctxs), seqs)
+        c_to = lax.rem(c + lax.rem(step, ctxs), ctxs)
+        at = pl.ds(pl.multiple_of((s_to * ctxs + c_to) * CAP, CAP), CAP)
+        remote(
+            packed.at[at], xall.at[0, mine], d_send.at[step], d_recv.at[step], {"seq": s_to, "ctx": c_to}
+        ).start()
+
+    xall[0, mine] = packed[mine]
+
+    for load in loads:
+        load.wait()
+    tail = jnp.zeros((width, padded - width), bf)
+    foot = jnp.zeros((padded - width, padded), bf)
+    for i in range(heads):
+        for j in range(2):
+            wgu[i, j * padded : j * padded + width, :] = jnp.concatenate(
+                [raw[j, :, i * width : (i + 1) * width], tail], axis=1
+            )
+            wgu[i, j * padded + width : (j + 1) * padded, :] = foot
+
+    def rows_of(g):
+        return pl.ds(pl.multiple_of(lax.rem(s + g, seqs) * block, block), block)
+
+    def gather(kind, g, source, target):
+        at = rows_of(g)
+        return remote(
+            xall.at[source, at],
+            xall.at[kind, at],
+            g_send.at[kind, g],
+            g_recv.at[kind, g],
+            {"head": target},
+        )
+
+    def stage_a(g):
+        @pl.loop(1 if g == 0 else 0, ctxs)
+        def _(dc):
+            step = g * ctxs + dc
+            at = pl.ds(0, CAP)
+            remote(
+                packed.at[at], xall.at[0, mine], d_send.at[step], d_recv.at[step], {"ctx": lax.rem(c + 1, ctxs)}
+            ).wait_recv()
+
+        gather(1, g, 0, other).start()
+        gather(2, g, 0, above).start()
+        gather(3, g, 0, below).start()
+
+    def stage_b(g):
+        gather(1, g, 0, other).wait_recv()
+        gather(4, g, 1, above).start()
+        gather(5, g, 1, below).start()
+        gather(2, g, 0, above).wait_recv()
+        gather(3, g, 0, below).wait_recv()
+        if g % 2 == 0:
+            gather(6, g, 2, above).start()
+        else:
+            gather(6, g, 3, below).start()
+
+    def stage_c(g):
+        gather(6, g, 2, above).wait_recv()
+        gather(7, g, 6, other).start()
+
+    place = [h, other, below, above, head_at(1, -1), head_at(1, 1), head_at(0, 2), head_at(1, 2)]
+
+    def absorb(low, high):
+        @pl.loop(low, high)
+        def _(kind):
+            where = place[low]
+            for k in range(low + 1, high):
+                where = jnp.where(kind == k, place[k], where)
+            update = lax.dot_general(xall[kind], wgu[where], NT, preferred_element_type=f32)
+            if low == 0:
+                acc[...] = update
+            else:
+                acc[...] += update
+
+    stage_a(0)
+    stage_a(1)
+    stage_b(0)
+    stage_a(2)
+    stage_b(1)
+    stage_c(0)
+    stage_a(3)
+    for i in range(heads):
+        wdn[i, 0:width, :] = jnp.concatenate([raw[2, :, i * width : (i + 1) * width], tail], axis=1)
+        wdn[i, width:padded, :] = foot
+    stage_b(2)
+    stage_c(1)
+    absorb(0, 1)
+    stage_b(3)
+    stage_c(2)
+    absorb(1, 4)
+    stage_c(3)
+    for g in range(GROUPS):
+        gather(4, g, 1, above).wait_recv()
+        gather(5, g, 1, below).wait_recv()
+    absorb(4, 7)
+    for g in range(GROUPS):
+        gather(7, g, 6, other).wait_recv()
+    absorb(7, 8)
+
+    @pl.loop(0, GROUPS)
+    def _(g):
+        at = pl.ds(pl.multiple_of(g * block, block), block)
+        tile = jnp.zeros((block, 128), f32)
+        for k in range(heads):
+            tile = tile + xall[k, at, padded - 128 : padded].astype(f32)
+        spot = lax.broadcasted_iota(jnp.int32, (block, 128), 1) + (padded - 128)
+        tile = jnp.where((spot >= width) & (spot < width + 3), tile, 0.0)
+        power = jnp.sum(tile, axis=1, keepdims=True)
+        scale = lax.rsqrt(power / (width * heads) + 1e-05)
+        gate = acc[at, 0:padded] * scale
+        up = acc[at, padded : 2 * padded] * scale
+        hidden[at] = (gate * jax.nn.sigmoid(1.702 * gate) * (up + 1.0)).astype(bf)
+
+    def part(g, target):
+        return jnp.dot(hidden[rows_of(g)], wdn[target], preferred_element_type=f32)
+
+    def scatter(kind, g, target):
+        return remote(
+            sbuf.at[kind, g], rbuf.at[kind, g], s_send.at[kind, g], s_recv.at[kind, g], {"head": target}
+        )
+
+    def got(kind, g):
+        scatter(kind, g, other).wait_recv()
+        return rbuf[kind, g].astype(f32)
+
+    def send(kind, g, value, target):
+        sbuf[kind, g] = value.astype(bf)
+        scatter(kind, g, target).start()
+
+    @pl.loop(0, GROUPS + 3)
+    def _(t):
+        @pl.when(t < GROUPS)
+        def _():
+            g = t
+            even = lax.rem(g, 2) == 0
+            send(0, g, part(g, head_at(1, 2)), other)
+            send(1, g, part(g, head_at(1, -1)), below)
+            send(2, g, part(g, head_at(1, 1)), above)
+
+            @pl.when(even)
+            def _():
+                send(5, g, part(g, below), below)
+
+            @pl.when(jnp.logical_not(even))
+            def _():
+                send(6, g, part(g, above), above)
+
+        @pl.when((t >= 1) & (t < GROUPS + 1))
+        def _():
+            g = t - 1
+            even = lax.rem(g, 2) == 0
+            value = part(g, head_at(0, 2)) + got(0, g)
+            send(3, g, value, jnp.where(even, above, below))
+            value = part(g, other) + got(1, g) + got(2, g)
+            send(4, g, value, other)
+
+        @pl.when((t >= 2) & (t < GROUPS + 2))
+        def _():
+            g = t - 2
+            even = lax.rem(g, 2) == 0
+
+            @pl.when(even)
+            def _():
+                send(6, g, part(g, above) + got(3, g), above)
+
+            @pl.when(jnp.logical_not(even))
+            def _():
+                send(5, g, part(g, below) + got(3, g), below)
+
+        @pl.when(t >= 3)
+        def _():
+            g = t - 3
+            value = part(g, h) + got(4, g) + got(5, g) + got(6, g)
+            final[rows_of(g)] = value.astype(bf)
+            s_to = lax.rem(s + g, seqs)
+
+            @pl.loop(0, ctxs)
+            def _(dc):
+                @pl.when(g * ctxs + dc > 0)
+                def _():
+                    step = g * ctxs + dc
+                    c_to = lax.rem(c + dc, ctxs)
+                    at = pl.ds(pl.multiple_of((s_to * ctxs + c_to) * CAP, CAP), CAP)
+                    remote(
+                        final.at[at], back.at[mine], b_send.at[step], b_recv.at[step], {"seq": s_to, "ctx": c_to}
+                    ).start()
+
+    back[mine] = final[mine]
+
+    def returned(step):
+        at = pl.ds(0, CAP)
+        return remote(
+            final.at[at], back.at[mine], b_send.at[step], b_recv.at[step], {"ctx": lax.rem(c + 1, ctxs)}
+        )
+
+    @pl.loop(1, experts)
+    def _(step):
+        returned(step).wait_recv()
+
+    moe = jnp.zeros((count, padded), f32)
+    for factor in factors:
+        moe = moe + jnp.dot(factor, back[...], preferred_element_type=f32)
+    out_ref[...] = (resid + moe[:, 0:width]).astype(bf)
+
+    @pl.loop(1, experts)
+    def _(step):
+        at = pl.ds(0, CAP)
+        remote(
+            packed.at[at], xall.at[0, mine], d_send.at[step], d_recv.at[step], {"ctx": lax.rem(c + 1, ctxs)}
+        ).wait_send()
+        returned(step).wait_send()
+
+    for g in range(GROUPS):
+        for kind in range(1, heads):
+            gather(kind, g, 0, other).wait_send()
+        for kind in range(heads - 1):
+            scatter(kind, g, other).wait_send()
+
+
+def route(resid, gain, ids, weights, gate, up, down):
+    seqs, ctxs, heads = lax.axis_size("seq"), lax.axis_size("ctx"), lax.axis_size("head")
+    experts = seqs * ctxs
+    slots = experts * CAP
+    count, width = resid.shape
+    hidden, model = gate.shape
+    padded = -(-(width + 3) // 128) * 128
+    block = ctxs * CAP
+    bf, f32 = jnp.bfloat16, jnp.float32
+    vm = pl.BlockSpec(memory_space=pltpu.VMEM)
+    dma = pltpu.SemaphoreType.DMA
+    return pl.pallas_call(
+        expert_kernel,
+        out_shape=jax.ShapeDtypeStruct((count, width), bf),
+        in_specs=[vm] * 4 + [pl.BlockSpec(memory_space=pl.ANY)] * 3,
+        out_specs=vm,
+        scratch_shapes=[
+            pltpu.VMEM((3, hidden, model), bf),
+            pltpu.VMEM((count, padded), f32),
+            pltpu.VMEM((heads, 2 * padded, padded), bf),
+            pltpu.VMEM((heads, padded, padded), bf),
+            pltpu.VMEM((slots, padded), bf),
+            pltpu.VMEM((heads, slots, padded), bf),
+            pltpu.VMEM((slots, 2 * padded), f32),
+            pltpu.VMEM((slots, padded), bf),
+            pltpu.VMEM((heads - 1, GROUPS, block, padded), bf),
+            pltpu.VMEM((heads - 1, GROUPS, block, padded), bf),
+            pltpu.VMEM((slots, padded), bf),
+            pltpu.VMEM((slots, padded), bf),
+            dma((3,)),
+            dma((experts,)),
+            dma((experts,)),
+            dma((heads, GROUPS)),
+            dma((heads, GROUPS)),
+            dma((heads - 1, GROUPS)),
+            dma((heads - 1, GROUPS)),
+            dma((experts,)),
+            dma((experts,)),
+        ],
+        compiler_params=pltpu.CompilerParams(
+            collective_id=1, has_side_effects=True, vmem_limit_bytes=48 * 1024 * 1024
+        ),
+    )(resid, gain, ids, weights, gate, up, down)
 
 
 def body(
@@ -333,15 +689,13 @@
     down_weight,
 ):
     tokens = stream[0]
-    count = tokens.shape[0]
-    model = tokens.shape[1]
-    kv_local = cache_keys.shape[2]
-    head_dim = cache_keys.shape[3]
+    count, model = tokens.shape
+    kv_local, head_dim = cache_keys.shape[2:]
     group = query_weight.shape[1] // (kv_local * head_dim)
-    scale = 1.0 / math.sqrt(head_dim)
     heads = lax.axis_size("head")
     width = model // heads
     offset = lax.axis_index("head") * width
+    scale = 1.0 / math.sqrt(head_dim)
     query = jnp.dot(tokens, query_weight, preferred_element_type=jnp.float32).astype(jnp.bfloat16)
     query = query * jnp.bfloat16(scale)
     pairs = group * head_dim // 128
@@ -349,7 +703,8 @@
     fresh_keys = new_keys[0, :, 0, :]
     fresh_values = new_values[0, :, 0, :]
     own = lax.dynamic_slice_in_dim(tokens, offset, width, 1).astype(jnp.float32)
-    resid_own = attend(
+    gain = lax.dynamic_slice_in_dim(norm_gain, offset, width, 0)[None]
+    resid = attend(
         query,
         cache_keys[0, :, 0, :].T,
         cache_values[0, :, 0, :].T,
@@ -358,47 +713,16 @@
         own,
         out_weight.T.reshape(heads, width, out_weight.shape[0]),
     )
-    power = taken_together(jnp.sum(resid_own * resid_own, axis=-1), "head")
-    gain_own = lax.dynamic_slice_in_dim(norm_gain, offset, width, 0)
-    normed = (resid_own * lax.rsqrt(power[:, None] / model + 1e-05) * gain_own).astype(jnp.bfloat16)
-    experts = lax.axis_size("seq") * lax.axis_size("ctx")
-    slots = experts * CAP
-    chosen = expert_ids[0].reshape(-1)
-    onehot = (chosen[:, None] == lax.broadcasted_iota(jnp.int32, (1, experts), 1)).astype(jnp.int32)
-    before = jnp.cumsum(onehot, axis=0) - onehot
-    target = chosen * CAP + jnp.sum(before * onehot, axis=1)
-    matches = target[None, :] == lax.broadcasted_iota(jnp.int32, (slots, 1), 0)
-    select = jnp.sum(matches.astype(jnp.float32).reshape(slots, count, -1), axis=-1).astype(
-        jnp.bfloat16
+    mixed = route(
+        resid,
+        gain,
+        expert_ids[0],
+        expert_weights[0],
+        gate_weight[0].T,
+        up_weight[0].T,
+        down_weight[0],
     )
-    packed = jnp.dot(select, normed, preferred_element_type=jnp.float32).astype(jnp.bfloat16)
-    packed = packed.reshape(experts, CAP, normed.shape[1])
-    arrived = lax.all_to_all(packed, ("seq", "ctx"), split_axis=0, concat_axis=0, tiled=True)
-    rows = arrived.reshape(slots, normed.shape[1])
-    piece = lax.all_gather(rows, "head", axis=1, tiled=True)
-    gate_rows = gate_weight[0]
-    up_rows = up_weight[0]
-    gate = jnp.dot(piece, gate_rows, preferred_element_type=jnp.float32)
-    up = jnp.dot(piece, up_rows, preferred_element_type=jnp.float32)
-    hidden = (gate * jax.nn.sigmoid(1.702 * gate) * (up + 1.0)).astype(jnp.bfloat16)
-    columns = down_weight[0]
-    expert_out = sent_and_summed(
-        jnp.einsum("fd,rf->dr", columns, hidden, preferred_element_type=jnp.float32).astype(
-            jnp.bfloat16
-        ),
-        "head",
-        0,
-    ).astype(jnp.bfloat16)
-    returned = lax.all_to_all(expert_out, ("seq", "ctx"), split_axis=1, concat_axis=1, tiled=True)
-    spread_weights = jnp.where(matches.T, expert_weights[0].reshape(-1)[:, None], 0.0)
-    spread_weights = jnp.sum(spread_weights.reshape(count, -1, slots), axis=1)
-    moe = lax.dot_general(
-        spread_weights,
-        returned.astype(jnp.float32),
-        (((1,), (1,)), ((), ())),
-        precision=lax.Precision.HIGHEST,
-    )
-    return (resid_own + moe).astype(jnp.bfloat16)[None]
+    return mixed[None]
 
 
 def solution(mesh):

time: 223 us -> 134 us (0.60)
  Pallas kernels: 46.4 us -> 125 us
  blocking collectives: 62.1 us -> 0 us
  waiting for transfers between devices: 53.3 us -> 0 us
  starting transfers between devices: 17.4 us -> 0 us
  matrix products: 17.3 us -> 1.63 us
  between operations: 13.6 us -> 0.1 us
  other arithmetic: 5.37 us -> 2.46 us
    pallas_call x0 -> x1, Pallas kernels: none -> 78.4 us  [route(): pl.pallas_call(expert_kernel, out_shape=jax.ShapeDtypeStruct((count, widt...]
    all_to_all x2 -> x0, blocking collectives: 62.1 us -> none  [the longest x1 37.1 us: sent_and_summed(): lax.all_to_all(tiles, axis, split_axis=0, concat_axis=0, tiled=True)]
    all_gather x1 -> x0, waiting for transfers between devices: 36.6 us -> none  [body(): piece = lax.all_gather(rows, 'head', axis=1, tiled=True)]
    all_to_all x2 -> x0, starting transfers between devices: 17.4 us -> none  [the longest x1 14.1 us: body(): lax.all_to_all(expert_out, ('seq', 'ctx'), split_axis=1, concat_axis=1, t...]
    all_to_all x2 -> x0, waiting for transfers between devices: 16.6 us -> none  [the longest x1 14.1 us: body(): lax.all_to_all(expert_out, ('seq', 'ctx'), split_axis=1, concat_axis=1, t...]
    dot_general x4 -> x0, matrix products: 15.6 us -> none  [the longest x1 7.94 us: body(): jnp.einsum('fd,rf->dr', columns, hidden, preferred_element_type=jnp.float32)]
    reduce_sum x6 -> x0, other arithmetic: 3.56 us -> none  [the longest x1 2.41 us: sent_and_summed(): return arrived.astype(jnp.float32).sum(axis=0)]
    unnamed x17 -> x19, local copies, waits for them, and re-layouts: 0.88 us -> 4.04 us
  transfers between devices with their start and end apart: 3 -> 0, of which waited for: 3 -> 0; matrix products, arithmetic and copies ran while one was open for 1% -> 0% of each run, Pallas kernels for 0% -> 0%
where the time goes in v2:
time: 134 us
  Pallas kernels  125 us (93%)
  local copies, waits for them, and re-layouts  4.84 us (4%)
  other arithmetic  2.46 us (2%)
  matrix products  1.63 us (1%)
    pallas_call x1, Pallas kernels, route(): pl.pallas_call(expert_kernel, out_shape=jax.ShapeDtypeStruct((count, widt...  78.4 us
    pallas_call x1, Pallas kernels, attend(): pl.pallas_call(attention_kernel, out_shape=jax.ShapeDtypeStruct((count, w...  46.4 us
    unnamed x19, local copies, waits for them, and re-layouts  4.04 us

profile of v2, /device:TPU:1, one launch (start us, length us, event | category | flops | bytes accessed | tf_op | source)
XLA Modules:
  0.0 133.8 jit_solution(3262341211365324200)
XLA Ops:
  0.0 0.0 copy-start
  0.0 0.0 copy-start.4
  0.0 0.0 copy-start.1
  0.0 0.0 copy-start.5
  0.0 1.1 bitcast_convert_fusion.own_ref
  1.1 1.4 %pad_maximum_fusion = (bf16[64,128]{1,0:T(8,128)(2,1)S(1)}, bf16[64,128]{1,0:T(8,128)(2,1)S(1)}) fusion(bf16[64,64]{1,0:T(8,128)(2,1)} %bitcast.46, bf16[64,64]{1,0:T(8,128)(2,1)} %bitcast.47), kind=kLoop, calls=%fused_computation.6 | loop fusion | flops 65536 | bytes 49152 | tf_op jit(solution)/shard_map/concatenate | solution.py:711
  2.5 0.0 copy-done
  2.5 0.0 copy-start.6
  2.5 0.0 copy-start.7
  2.5 1.6 %fusion.1 = bf16[8,4,8,128]{3,2,1,0:T(8,128)(2,1)S(1)} fusion(bf16[2880,512]{1,0:T(8,128)(2,1)S(1)} %copy-done, bf16[1,64,2880]{2,1,0:T(8,128)(2,1)} %param.13), kind=kOutput, calls=%fused_computation.2 | convolution fusion | flops 188809216 | bytes 3383296 | tf_op jit(solution)/shard_map/dot_general | solution.py:699
  4.2 0.0 copy-done.4
  4.2 0.0 copy-done.1
  4.2 0.0 copy-done.5
  4.2 46.4 %shard_map.127.resid_ref = f32[64,360]{1,0:T(8,128)S(1)} custom-call(bf16[256,128]{1,0:T(8,128)(2,1)S(1)} %bitcast.41, bf16[64,2048]{1,0:T(8,128)(2,1)S(1)} %bitcast.39, bf16[64,2048]{1,0:T(8,128)(2,1)S(1)} %bitcast.40, bf16[64,128]{1,0:T(8,128)(2,1)S(1)} %get-tuple-element.5.nk_ref, bf16[64,128]{1,0:T(8,128)(2,1)S(1)} %get-tuple-element.6.nv_ref, ...), custom_call_target="tpu_custom_call" | custom-call | tf_op jit(solution)/shard_map/pallas_call | solution.py:253
  50.6 0.8 dynamic_slice.7
  51.4 0.0 copy-done.6
  51.4 0.1 copy.15
  51.5 0.0 copy-done.7
  51.5 0.1 copy.16
  51.6 0.0 copy-start.2
  51.6 1.6 %copy-done.2 = bf16[1,2880,360]{1,2,0:T(8,128)(2,1)S(1)} copy-done((bf16[1,2880,360]{1,2,0:T(8,128)(2,1)S(1)}, bf16[1,2880,360]{1,2,0:T(8,128)(2,1)}, u32[]{:S(2)}) %copy-start.2) | copy-done | bytes 2073624
  53.2 1.6 %copy-done.3 = bf16[1,2880,360]{1,2,0:T(8,128)(2,1)S(1)} copy-done((bf16[1,2880,360]{1,2,0:T(8,128)(2,1)S(1)}, bf16[1,2880,360]{1,2,0:T(8,128)(2,1)}, u32[]{:S(2)}) %copy-start.3) | copy-done | bytes 2073624
  54.8 78.4 %shard_map.128 = bf16[64,360]{1,0:T(8,128)(2,1)S(1)} custom-call(f32[64,360]{1,0:T(8,128)S(1)} %shard_map.127.resid_ref, f32[1,360]{1,0:T(1,128)S(1)} %broadcast_in_dim.6.gain_ref, s32[64,4]{1,0:T(8,128)S(1)} %bitcast.43, f32[64,4]{1,0:T(8,128)S(1)} %bitcast.44, bf16[360,2880]{1,0:T(8,128)(2,1)S(1)} %bitcast.37, bf16[360,2880]{1,0:T(8,128)(2,1)S(1)} %bitcast.38, ...), custom_call_target="tpu_custom_call" | custom-call | tf_op jit(solution)/shard_map/pallas_call | solution.py:642
  133.2 0.6 copy.21
  (3 shorter events, 0.0 us)
Async XLA Ops:
  0.0 2.5 %copy-start = (bf16[2880,512]{1,0:T(8,128)(2,1)S(1)}, bf16[2880,512]{1,0:T(8,128)(2,1)}, u32[]{:S(2)}) copy-start(bf16[2880,512]{1,0:T(8,128)(2,1)} %param.14) | copy-start | bytes 8847364
  0.0 4.2 %copy-start.4 = (bf16[1,2048,1,64]{1,3,2,0:T(8,128)(2,1)S(1)}, bf16[1,2048,1,64]{1,3,2,0:T(8,128)(2,1)}, u32[]{:S(2)}) copy-start(bf16[1,2048,1,64]{1,3,2,0:T(8,128)(2,1)} %param.15) | copy-start | bytes 786436
  0.0 4.2 %copy-start.1 = (bf16[512,2880]{0,1:T(8,128)(2,1)S(1)}, bf16[512,2880]{0,1:T(8,128)(2,1)}, u32[]{:S(2)}) copy-start(bf16[512,2880]{0,1:T(8,128)(2,1)} %param.19) | copy-start | bytes 8847364
  0.0 4.2 %copy-start.5 = (bf16[1,2048,1,64]{1,3,2,0:T(8,128)(2,1)S(1)}, bf16[1,2048,1,64]{1,3,2,0:T(8,128)(2,1)}, u32[]{:S(2)}) copy-start(bf16[1,2048,1,64]{1,3,2,0:T(8,128)(2,1)} %param.16) | copy-start | bytes 786436
  2.5 48.9 %copy-start.6 = (s32[1,64,4]{1,2,0:T(4,128)S(1)}, s32[1,64,4]{1,2,0:T(4,128)}, u32[]{:S(2)}) copy-start(s32[1,64,4]{1,2,0:T(4,128)} %param.21) | copy-start | bytes 3076
  2.5 49.0 %copy-start.7 = (f32[1,64,4]{1,2,0:T(4,128)S(1)}, f32[1,64,4]{1,2,0:T(4,128)}, u32[]{:S(2)}) copy-start(f32[1,64,4]{1,2,0:T(4,128)} %param.22) | copy-start | bytes 3076
  51.6 1.6 %copy-start.2 = (bf16[1,2880,360]{1,2,0:T(8,128)(2,1)S(1)}, bf16[1,2880,360]{1,2,0:T(8,128)(2,1)}, u32[]{:S(2)}) copy-start(bf16[1,2880,360]{1,2,0:T(8,128)(2,1)} %param.23) | copy-start | bytes 6220804
  53.2 1.6 %copy-start.3 = (bf16[1,2880,360]{1,2,0:T(8,128)(2,1)S(1)}, bf16[1,2880,360]{1,2,0:T(8,128)(2,1)}, u32[]{:S(2)}) copy-start(bf16[1,2880,360]{1,2,0:T(8,128)(2,1)} %param.24) | copy-start | bytes 6220804

commit v3 on v2

v3 whole, which is shorter than its diff:
```python
import math

import jax
import jax.numpy as jnp
from jax import lax
from jax.experimental import pallas as pl
from jax.experimental.pallas import tpu as pltpu
from jax.sharding import PartitionSpec as P

CAP = 16
MESH = pl.DeviceIdType.MESH
LOG2E = 1.4426950408889634
NEG = -3.0e38
NT = (((1,), (1,)), ((), ()))
GROUPS = 4
DEPTH = 768


def remote(src, dst, send, recv, where):
    return pltpu.make_async_remote_copy(
        src_ref=src, dst_ref=dst, send_sem=send, recv_sem=recv, device_id=where, device_id_type=MESH
    )


def layer_kernel(
    tok_hbm,
    qw_hbm,
    kt_hbm,
    vt_hbm,
    nk_ref,
    nv_ref,
    wo_hbm,
    gain_ref,
    ids_ref,
    weights_ref,
    gate_hbm,
    up_hbm,
    down_hbm,
    out_ref,
    tok,
    qw,
    vt,
    own,
    gain,
    resid_s,
    qbuf,
    ke,
    ko,
    ve,
    vo,
    kn,
    vn,
    s_low,
    s_high,
    s_new,
    tops,
    level,
    p_new,
    half_acc,
    obuf,
    lbuf,
    rbuf_o,
    rlse,
    wo,
    pbuf,
    prec,
    raw,
    wide,
    wgu,
    wdn,
    select_s,
    factor_s,
    packed,
    xall,
    acc,
    hidden,
    sbuf,
    rbuf,
    final,
    back,
    in_sem,
    q_send,
    q_recv,
    o_send,
    o_recv,
    l_send,
    l_recv,
    p_send,
    p_recv,
    w_sem,
    d_send,
    d_recv,
    g_send,
    g_recv,
    s_send,
    s_recv,
    b_send,
    b_recv,
):
    seqs, ctxs, heads = lax.axis_size("seq"), lax.axis_size("ctx"), lax.axis_size("head")
    s, c, h = lax.axis_index("seq"), lax.axis_index("ctx"), lax.axis_index("head")
    n, place, lane_of = ctxs, c, h
    experts = seqs * ctxs
    count, model = tok.shape
    width = own.shape[1]
    padded = wide.shape[1]
    block = ctxs * CAP
    f32, bf = jnp.float32, jnp.bfloat16
    ring = heads // 2
    col, y = lax.div(h, ring), lax.rem(h, ring)
    rows = qbuf.shape[1]
    half = ke.shape[0] // 2
    cached = ke.shape[1]
    pair = 2 * half

    def head_at(across, dy):
        return (col if across == 0 else 1 - col) * ring + lax.rem(y + dy + ring, ring)

    other, above, below = head_at(1, 0), head_at(0, 1), head_at(0, -1)
    edges = list(range(0, model, DEPTH)) + [model]
    spans = list(zip(edges[:-1], edges[1:]))
    tok_load = pltpu.make_async_copy(tok_hbm, tok, in_sem.at[0])
    qw_loads = [
        pltpu.make_async_copy(qw_hbm.at[low:high], qw.at[low:high], in_sem.at[4 + i])
        for i, (low, high) in enumerate(spans)
    ]
    kv_loads = [
        pltpu.make_async_copy(kt_hbm, ke.at[0:half], in_sem.at[1]),
        pltpu.make_async_copy(kt_hbm, ko.at[half:pair], in_sem.at[2]),
        pltpu.make_async_copy(vt_hbm, vt, in_sem.at[3]),
    ]
    for load in [tok_load] + qw_loads + kv_loads:
        load.start()
    wo_copy = pltpu.make_async_copy(wo_hbm, wo, w_sem.at[3])
    loads = [
        pltpu.make_async_copy(source, raw.at[i], w_sem.at[i])
        for i, source in enumerate((gate_hbm, up_hbm, down_hbm))
    ]
    barrier = pltpu.get_barrier_semaphore()

    @pl.loop(1, experts)
    def _(step):
        there = {
            "seq": lax.rem(s + lax.div(step, ctxs), seqs),
            "ctx": lax.rem(c + lax.rem(step, ctxs), ctxs),
        }
        pl.semaphore_signal(barrier, inc=1, device_id=there, device_id_type=MESH)

    @pl.loop(1, heads)
    def _(step):
        there = {"head": lax.rem(h + step, heads)}
        pl.semaphore_signal(barrier, inc=1, device_id=there, device_id_type=MESH)

    ke[half:pair, :] = jnp.zeros((half, cached), bf)
    ko[0:half, :] = jnp.zeros((half, cached), bf)
    low_n = lax.broadcasted_iota(jnp.int32, (count, pair), 1) < half
    nk = nk_ref[...].astype(f32)
    nk = jnp.concatenate([nk, nk], axis=1)
    nv = nv_ref[...].astype(f32)
    nv = jnp.concatenate([nv, nv], axis=1)
    kn[0:count, :] = jnp.where(low_n, nk, 0.0).astype(bf)
    kn[count : 2 * count, :] = jnp.where(low_n, 0.0, nk).astype(bf)
    vn[0:count, 0:pair] = jnp.where(low_n, nv, 0.0).astype(bf)
    vn[count : 2 * count, 0:pair] = jnp.where(low_n, 0.0, nv).astype(bf)
    vn[0:count, pair : 2 * pair] = jnp.where(low_n, 1.0, 0.0).astype(bf)
    vn[count : 2 * count, pair : 2 * pair] = jnp.where(low_n, 0.0, 1.0).astype(bf)

    tok_load.wait()
    query = jnp.zeros((count, qw.shape[1]), f32)
    for (low_k, high_k), load in zip(spans, qw_loads):
        load.wait()
        query = query + jnp.dot(tok[:, low_k:high_k], qw[low_k:high_k, :], preferred_element_type=f32)
    query = (query.astype(bf).astype(f32) * (1.0 / math.sqrt(half))).astype(bf)
    for j in range(rows // count):
        qbuf[0, count * j : count * (j + 1), :] = query[:, pair * j : pair * (j + 1)]
    for load in kv_loads:
        load.wait()

    pl.semaphore_wait(barrier, experts - 1 + heads - 1)
    right = lax.rem(place + 1, n)
    left = lax.rem(place + n - 1, n)
    remote(qbuf.at[0], qbuf.at[1], q_send.at[1], q_recv.at[1], {"ctx": right}).start()
    remote(qbuf.at[0], qbuf.at[2], q_send.at[2], q_recv.at[2], {"ctx": left}).start()
    wo_copy.start()
    for load in loads:
        load.start()

    span = 256

    @pl.loop(0, cached // span)
    def _(i):
        at = pl.ds(pl.multiple_of(i * span, span), span)
        ones = jnp.where(lax.broadcasted_iota(jnp.int32, (span, pair), 1) < half, 1.0, 0.0)
        v = vt[:, at].astype(f32)
        blank = jnp.zeros_like(v)
        ve[at, 0:pair] = jnp.concatenate([v, blank], 0).T.astype(bf)
        vo[at, 0:pair] = jnp.concatenate([blank, v], 0).T.astype(bf)
        ve[at, pair : 2 * pair] = ones.astype(bf)
        vo[at, pair : 2 * pair] = (1.0 - ones).astype(bf)

    lane = lax.broadcasted_iota(jnp.int32, (rows, pair), 1)
    low = lane < half
    tokpos = lax.rem(lax.broadcasted_iota(jnp.int32, (rows, pair), 0), count)
    pos = lax.rem(lane, half)

    def source_of(k):
        return lax.rem(place + lax.div(k + 1, 2) * (1 - 2 * lax.rem(k, 2)) + n, n)

    def score_even(k, turn):
        q = qbuf[k]
        source = source_of(k)
        fresh = lax.dot_general(q, kn[...], NT, preferred_element_type=f32)
        ahead = jnp.where(place < source, count, jnp.where(place == source, 0, -count - 1))
        fresh = jnp.where(pos <= tokpos + ahead, fresh, NEG)
        s_new[turn] = fresh
        score = jnp.dot(q, ke[...], preferred_element_type=f32)
        s_low[...] = score
        peak = jnp.maximum(
            jnp.max(score, axis=1, keepdims=True),
            jnp.max(jnp.where(low, fresh, NEG), axis=1, keepdims=True),
        )
        tops[turn] = jnp.broadcast_to(peak, (rows, pair))

    score_even(0, 0)

    @pl.loop(0, n)
    def _(k):
        turn = lax.rem(k, 2)
        score = jnp.dot(qbuf[k], ko[...], preferred_element_type=f32)
        s_high[...] = score
        m_e = tops[turn]
        p_e = jnp.exp2((s_low[...] - m_e[:, 0:1]) * LOG2E).astype(bf)
        half_acc[...] = jnp.dot(p_e, ve[...], preferred_element_type=f32)
        m_o = jnp.maximum(
            jnp.max(score, axis=1, keepdims=True),
            jnp.max(jnp.where(low, NEG, s_new[turn]), axis=1, keepdims=True),
        )
        both = jnp.where(low, m_e, m_o)
        level[...] = both
        p_new[...] = jnp.exp2((s_new[turn] - both) * LOG2E).astype(bf)

        @pl.when(k + 1 < n)
        def _():
            remote(
                qbuf.at[k + 1], qbuf.at[k + 1], q_send.at[k + 1], q_recv.at[k + 1], {"ctx": right}
            ).wait_recv()

            @pl.when(k + 3 < n)
            def _():
                onward = lax.rem(place + n + 1 - 2 * lax.rem(k, 2), n)
                remote(
                    qbuf.at[k + 1],
                    qbuf.at[k + 3],
                    q_send.at[k + 3],
                    q_recv.at[k + 3],
                    {"ctx": onward},
                ).start()

        score_even(jnp.minimum(k + 1, n - 1), 1 - turn)
        both = level[...]
        p_o = jnp.exp2((s_high[...] - both[:, half : half + 1]) * LOG2E).astype(bf)
        whole = (
            half_acc[...]
            + jnp.dot(p_o, vo[...], preferred_element_type=f32)
            + jnp.dot(p_new[...], vn[...], preferred_element_type=f32)
        )
        num = whole[:, 0:pair]
        tot = whole[:, pair : 2 * pair]
        obuf[k] = (num / tot).astype(bf)
        turned = (both + jnp.log(tot)).T
        first = lax.broadcasted_iota(jnp.int32, (8, rows), 0) < 4
        lbuf[k] = jnp.where(first, turned[0:8, :], turned[half : half + 8, :])

        @pl.when(k > 0)
        def _():
            there = {"ctx": source_of(k)}
            remote(obuf.at[k], rbuf_o.at[k], o_send.at[k], o_recv.at[k], there).start()
            remote(lbuf.at[k], rlse.at[k], l_send.at[k], l_recv.at[k], there).start()

    for i in range(heads):

        @pl.when(h == i)
        def _():
            own[...] = tok[:, i * width : (i + 1) * width].astype(f32)
            gain[...] = gain_ref[:, i * width : (i + 1) * width]

    ids = ids_ref[...]
    given = weights_ref[...]
    index = lax.broadcasted_iota(jnp.int32, (count, experts), 1)
    named = jnp.zeros((count, experts), f32)
    amount = jnp.zeros((count, experts), f32)
    for j in range(ids.shape[1]):
        hit = ids[:, j : j + 1] == index
        named = named + jnp.where(hit, 1.0, 0.0)
        amount = amount + jnp.where(hit, given[:, j : j + 1], 0.0)
    before = jnp.where(
        lax.broadcasted_iota(jnp.int32, (count, count), 1)
        < lax.broadcasted_iota(jnp.int32, (count, count), 0),
        1.0,
        0.0,
    ).astype(bf)
    rank = jnp.dot(before, named.astype(bf), preferred_element_type=f32)
    key = jnp.where(named > 0.5, rank, 128.0)
    spread = jnp.where(
        lax.div(lax.broadcasted_iota(jnp.int32, (experts, experts * CAP), 1), CAP)
        == lax.broadcasted_iota(jnp.int32, (experts, experts * CAP), 0),
        1.0,
        0.0,
    ).astype(bf)
    key = jnp.dot(key.astype(bf), spread, preferred_element_type=f32)
    slot = lax.rem(lax.broadcasted_iota(jnp.int32, (count, experts * CAP), 1), CAP).astype(f32)
    chosen = key == slot
    select_s[...] = jnp.where(chosen, 1.0, 0.0).T.astype(bf)

    def pieces(x):
        one = x.astype(bf)
        rest = x - one.astype(f32)
        two = rest.astype(bf)
        return one, two, (rest - two.astype(f32)).astype(bf)

    for i, piece in enumerate(pieces(amount)):
        on_slots = jnp.dot(piece, spread, preferred_element_type=f32)
        factor_s[i] = jnp.where(chosen, on_slots, 0.0).astype(bf)

    for load in loads:
        load.wait()
    tail = jnp.zeros((width, padded - width), bf)
    foot = jnp.zeros((padded - width, padded), bf)
    for i in range(heads):
        for j in range(2):
            wgu[i, j * padded : j * padded + width, :] = jnp.concatenate(
                [raw[j, :, i * width : (i + 1) * width], tail], axis=1
            )
            wgu[i, j * padded + width : (j + 1) * padded, :] = foot
        wdn[i, 0:width, :] = jnp.concatenate([raw[2, :, i * width : (i + 1) * width], tail], axis=1)
        wdn[i, width:padded, :] = foot
    wo_copy.wait()

    @pl.loop(1, n)
    def _(k):
        here = {"ctx": right}
        remote(obuf.at[k], rbuf_o.at[k], o_send.at[k], o_recv.at[k], here).wait_recv()
        remote(lbuf.at[k], rlse.at[k], l_send.at[k], l_recv.at[k], here).wait_recv()

    rbuf_o[0] = obuf[0]
    rlse[0] = lbuf[0]
    lse = [rlse[k] for k in range(n)]
    peak = lse[0]
    for k in range(1, n):
        peak = jnp.maximum(peak, lse[k])
    parts = [jnp.exp(x - peak) for x in lse]
    whole = parts[0]
    for k in range(1, n):
        whole = whole + parts[k]
    share = jnp.concatenate([x / whole for x in parts], axis=0)
    share = jnp.concatenate([share, share], axis=0).T
    upper = share.astype(bf).astype(f32)
    first = lax.broadcasted_iota(jnp.int32, share.shape, 1) < 8 * n
    split = jnp.where(first, upper, share - upper).astype(bf)
    spot = lax.broadcasted_iota(jnp.int32, (16 * n, pair * n), 1)
    line = lax.broadcasted_iota(jnp.int32, (16 * n, pair * n), 0)
    wanted = lax.div(spot, pair) * 8 + jnp.where(lax.rem(spot, pair) < half, 0, 4)
    pick = jnp.where(lax.rem(line, 8 * n) == wanted, 1.0, 0.0).astype(bf)
    factor = jnp.dot(split, pick, preferred_element_type=f32)
    attn = jnp.zeros((rows, pair), f32)
    for k in range(n):
        attn = attn + factor[:, pair * k : pair * (k + 1)] * rbuf_o[k].astype(f32)
    attn = attn.astype(bf)
    flat = jnp.concatenate([attn[count * j : count * (j + 1), :] for j in range(rows // count)], axis=1)

    @pl.loop(0, heads - 1)
    def _(i):
        there = lax.rem(lane_of + 1 + i, heads)
        part = lax.dot_general(flat, wo[there], NT, preferred_element_type=f32)
        pbuf[i] = part.astype(bf)
        remote(pbuf.at[i], prec.at[i], p_send.at[i], p_recv.at[i], {"head": there}).start()

    mine = lax.dot_general(flat, wo[lane_of], NT, preferred_element_type=f32)
    total = own[...] + mine
    for i in range(heads - 1):
        there = lax.rem(lane_of + 1 + i, heads)
        remote(pbuf.at[i], prec.at[i], p_send.at[i], p_recv.at[i], {"head": there}).wait_recv()
        total = total + prec[i].astype(f32)
    resid_s[...] = total

    resid = resid_s[...]
    wide[...] = jnp.zeros(wide.shape, f32)
    wide[:, 0:width] = resid * gain[...]
    power = jnp.sum(resid * resid, axis=1, keepdims=True)
    lane = lax.broadcasted_iota(jnp.int32, (count, padded), 1)
    row = wide[...]
    for i, piece in enumerate(pieces(power)):
        row = jnp.where(lane == width + i, piece.astype(f32), row)
    packed[...] = jnp.dot(select_s[...], row.astype(bf), preferred_element_type=f32).astype(bf)

    me = s * ctxs + c
    mine = pl.ds(pl.multiple_of(me * CAP, CAP), CAP)

    @pl.loop(1, experts)
    def _(step):
        s_to = lax.rem(s + seqs - lax.div(step, ctxs), seqs)
        c_to = lax.rem(c + lax.rem(step, ctxs), ctxs)
        at = pl.ds(pl.multiple_of((s_to * ctxs + c_to) * CAP, CAP), CAP)
        remote(
            packed.at[at], xall.at[0, mine], d_send.at[step], d_recv.at[step], {"seq": s_to, "ctx": c_to}
        ).start()

    xall[0, mine] = packed[mine]

    def rows_of(g):
        return pl.ds(pl.multiple_of(lax.rem(s + g, seqs) * block, block), block)

    def gather(kind, g, source, target):
        at = rows_of(g)
        return remote(
            xall.at[source, at],
            xall.at[kind, at],
            g_send.at[kind, g],
            g_recv.at[kind, g],
            {"head": target},
        )

    def stage_a(g):
        @pl.loop(1 if g == 0 else 0, ctxs)
        def _(dc):
            step = g * ctxs + dc
            at = pl.ds(0, CAP)
            remote(
                packed.at[at], xall.at[0, mine], d_send.at[step], d_recv.at[step], {"ctx": lax.rem(c + 1, ctxs)}
            ).wait_recv()

        gather(1, g, 0, other).start()
        gather(2, g, 0, above).start()
        gather(3, g, 0, below).start()

    def stage_b(g):
        gather(1, g, 0, other).wait_recv()
        gather(4, g, 1, above).start()
        gather(5, g, 1, below).start()
        gather(2, g, 0, above).wait_recv()
        gather(3, g, 0, below).wait_recv()
        if g % 2 == 0:
            gather(6, g, 2, above).start()
        else:
            gather(6, g, 3, below).start()

    def stage_c(g):
        gather(6, g, 2, above).wait_recv()
        gather(7, g, 6, other).start()

    slabs = [h, other, below, above, head_at(1, -1), head_at(1, 1), head_at(0, 2), head_at(1, 2)]

    def absorb(low, high):
        @pl.loop(low, high)
        def _(kind):
            where = slabs[low]
            for k in range(low + 1, high):
                where = jnp.where(kind == k, slabs[k], where)
            update = lax.dot_general(xall[kind], wgu[where], NT, preferred_element_type=f32)
            if low == 0:
                acc[...] = update
            else:
                acc[...] += update

    stage_a(0)
    stage_a(1)
    stage_b(0)
    stage_a(2)
    stage_b(1)
    stage_c(0)
    stage_a(3)
    stage_b(2)
    stage_c(1)
    absorb(0, 1)
    stage_b(3)
    stage_c(2)
    absorb(1, 4)
    stage_c(3)
    for g in range(GROUPS):
        gather(4, g, 1, above).wait_recv()
        gather(5, g, 1, below).wait_recv()
    absorb(4, 7)
    for g in range(GROUPS):
        gather(7, g, 6, other).wait_recv()
    absorb(7, 8)

    @pl.loop(0, GROUPS)
    def _(g):
        at = pl.ds(pl.multiple_of(g * block, block), block)
        tile = jnp.zeros((block, 128), f32)
        for k in range(heads):
            tile = tile + xall[k, at, padded - 128 : padded].astype(f32)
        spot = lax.broadcasted_iota(jnp.int32, (block, 128), 1) + (padded - 128)
        tile = jnp.where((spot >= width) & (spot < width + 3), tile, 0.0)
        power = jnp.sum(tile, axis=1, keepdims=True)
        scale = lax.rsqrt(power / (width * heads) + 1e-05)
        gate = acc[at, 0:padded] * scale
        up = acc[at, padded : 2 * padded] * scale
        hidden[at] = (gate * jax.nn.sigmoid(1.702 * gate) * (up + 1.0)).astype(bf)

    def part(g, target):
        return jnp.dot(hidden[rows_of(g)], wdn[target], preferred_element_type=f32)

    def scatter(kind, g, target):
        return remote(
            sbuf.at[kind, g], rbuf.at[kind, g], s_send.at[kind, g], s_recv.at[kind, g], {"head": target}
        )

    def got(kind, g):
        scatter(kind, g, other).wait_recv()
        return rbuf[kind, g].astype(f32)

    def send(kind, g, value, target):
        sbuf[kind, g] = value.astype(bf)
        scatter(kind, g, target).start()

    @pl.loop(0, GROUPS + 4)
    def _(t):
        @pl.when(t < GROUPS)
        def _():
            g = t
            even = lax.rem(g, 2) == 0
            send(0, g, part(g, head_at(1, 2)), other)
            send(1, g, part(g, head_at(1, -1)), below)
            send(2, g, part(g, head_at(1, 1)), above)

            @pl.when(even)
            def _():
                send(5, g, part(g, below), below)

            @pl.when(jnp.logical_not(even))
            def _():
                send(6, g, part(g, above), above)

        @pl.when((t >= 2) & (t < GROUPS + 2))
        def _():
            g = t - 2
            even = lax.rem(g, 2) == 0
            value = part(g, head_at(0, 2)) + got(0, g)
            send(3, g, value, jnp.where(even, above, below))
            value = part(g, other) + got(1, g) + got(2, g)
            send(4, g, value, other)

        @pl.when((t >= 3) & (t < GROUPS + 3))
        def _():
            g = t - 3
            even = lax.rem(g, 2) == 0

            @pl.when(even)
            def _():
                send(6, g, part(g, above) + got(3, g), above)

            @pl.when(jnp.logical_not(even))
            def _():
                send(5, g, part(g, below) + got(3, g), below)

        @pl.when(t >= 4)
        def _():
            g = t - 4
            value = part(g, h) + got(4, g) + got(5, g) + got(6, g)
            final[rows_of(g)] = value.astype(bf)
            s_to = lax.rem(s + g, seqs)

            @pl.loop(0, ctxs)
            def _(dc):
                @pl.when(g * ctxs + dc > 0)
                def _():
                    step = g * ctxs + dc
                    c_to = lax.rem(c + dc, ctxs)
                    at = pl.ds(pl.multiple_of((s_to * ctxs + c_to) * CAP, CAP), CAP)
                    remote(
                        final.at[at], back.at[mine], b_send.at[step], b_recv.at[step], {"seq": s_to, "ctx": c_to}
                    ).start()

    back[mine] = final[mine]

    def returned(step):
        at = pl.ds(0, CAP)
        return remote(
            final.at[at], back.at[mine], b_send.at[step], b_recv.at[step], {"ctx": lax.rem(c + 1, ctxs)}
        )

    @pl.loop(1, experts)
    def _(step):
        returned(step).wait_recv()

    moe = jnp.zeros((count, padded), f32)
    for i in range(3):
        moe = moe + jnp.dot(factor_s[i], back[...], preferred_element_type=f32)
    out_ref[...] = (resid_s[...] + moe[:, 0:width]).astype(bf)

    @pl.loop(1, experts)
    def _(step):
        at = pl.ds(0, CAP)
        remote(
            packed.at[at], xall.at[0, mine], d_send.at[step], d_recv.at[step], {"ctx": lax.rem(c + 1, ctxs)}
        ).wait_send()
        returned(step).wait_send()

    for g in range(GROUPS):
        for kind in range(1, heads):
            gather(kind, g, 0, other).wait_send()
        for kind in range(heads - 1):
            scatter(kind, g, other).wait_send()

    @pl.loop(1, n)
    def _(k):
        here = {"ctx": right}
        remote(qbuf.at[k], qbuf.at[k], q_send.at[k], q_recv.at[k], here).wait_send()
        remote(obuf.at[k], rbuf_o.at[k], o_send.at[k], o_recv.at[k], here).wait_send()
        remote(lbuf.at[k], rlse.at[k], l_send.at[k], l_recv.at[k], here).wait_send()

    @pl.loop(0, heads - 1)
    def _(c):
        there = lax.rem(lane_of + 1 + c, heads)
        remote(pbuf.at[c], prec.at[c], p_send.at[c], p_recv.at[c], {"head": there}).wait_send()


def layer(tokens, qw, kt, vt, nk, nv, wo, gain, ids, weights, gate, up, down):
    seqs, ctxs, heads = lax.axis_size("seq"), lax.axis_size("ctx"), lax.axis_size("head")
    experts = seqs * ctxs
    slots = experts * CAP
    count, model = tokens.shape
    width = model // heads
    half, cached = kt.shape
    pair = 2 * half
    rows = qw.shape[1] // pair * count
    hidden = gate.shape[0]
    padded = -(-(width + 3) // 128) * 128
    block = ctxs * CAP
    bf, f32 = jnp.bfloat16, jnp.float32
    vm = pl.BlockSpec(memory_space=pltpu.VMEM)
    hbm = pl.BlockSpec(memory_space=pl.ANY)
    dma = pltpu.SemaphoreType.DMA
    spans = -(-model // DEPTH)
    return pl.pallas_call(
        layer_kernel,
        out_shape=jax.ShapeDtypeStruct((count, width), bf),
        in_specs=[hbm] * 4 + [vm] * 2 + [hbm] + [vm] * 3 + [hbm] * 3,
        out_specs=vm,
        scratch_shapes=[
            pltpu.VMEM((count, model), bf),
            pltpu.VMEM(qw.shape, bf),
            pltpu.VMEM(vt.shape, bf),
            pltpu.VMEM((count, width), f32),
            pltpu.VMEM((1, width), f32),
            pltpu.VMEM((count, width), f32),
            pltpu.VMEM((ctxs, rows, pair), bf),
            pltpu.VMEM((pair, cached), bf),
            pltpu.VMEM((pair, cached), bf),
            pltpu.VMEM((cached, 2 * pair), bf),
            pltpu.VMEM((cached, 2 * pair), bf),
            pltpu.VMEM((2 * count, pair), bf),
            pltpu.VMEM((2 * count, 2 * pair), bf),
            pltpu.VMEM((rows, cached), f32),
            pltpu.VMEM((rows, cached), f32),
            pltpu.VMEM((2, rows, pair), f32),
            pltpu.VMEM((2, rows, pair), f32),
            pltpu.VMEM((rows, pair), f32),
            pltpu.VMEM((rows, pair), bf),
            pltpu.VMEM((rows, 2 * pair), f32),
            pltpu.VMEM((ctxs, rows, pair), bf),
            pltpu.VMEM((ctxs, 8, rows), f32),
            pltpu.VMEM((ctxs, rows, pair), bf),
            pltpu.VMEM((ctxs, 8, rows), f32),
            pltpu.VMEM(wo.shape, bf),
            pltpu.VMEM((heads - 1, count, width), bf),
            pltpu.VMEM((heads - 1, count, width), bf),
            pltpu.VMEM((3, hidden, model), bf),
            pltpu.VMEM((count, padded), f32),
            pltpu.VMEM((heads, 2 * padded, padded), bf),
            pltpu.VMEM((heads, padded, padded), bf),
            pltpu.VMEM((slots, count), bf),
            pltpu.VMEM((3, count, slots), bf),
            pltpu.VMEM((slots, padded), bf),
            pltpu.VMEM((heads, slots, padded), bf),
            pltpu.VMEM((slots, 2 * padded), f32),
            pltpu.VMEM((slots, padded), bf),
            pltpu.VMEM((heads - 1, GROUPS, block, padded), bf),
            pltpu.VMEM((heads - 1, GROUPS, block, padded), bf),
            pltpu.VMEM((slots, padded), bf),
            pltpu.VMEM((slots, padded), bf),
            dma((4 + spans,)),
            dma((ctxs,)),
            dma((ctxs,)),
            dma((ctxs,)),
            dma((ctxs,)),
            dma((ctxs,)),
            dma((ctxs,)),
            dma((heads - 1,)),
            dma((heads - 1,)),
            dma((4,)),
            dma((experts,)),
            dma((experts,)),
            dma((heads, GROUPS)),
            dma((heads, GROUPS)),
            dma((heads - 1, GROUPS)),
            dma((heads - 1, GROUPS)),
            dma((experts,)),
            dma((experts,)),
        ],
        compiler_params=pltpu.CompilerParams(
            collective_id=0, has_side_effects=True, vmem_limit_bytes=60 * 1024 * 1024
        ),
    )(tokens, qw, kt, vt, nk, nv, wo, gain, ids, weights, gate, up, down)


def body(
    stream,
    query_weight,
    cache_keys,
    cache_values,
    new_keys,
    new_values,
    out_weight,
    norm_gain,
    expert_ids,
    expert_weights,
    gate_weight,
    up_weight,
    down_weight,
):
    heads = lax.axis_size("head")
    taken, model = out_weight.shape
    mixed = layer(
        stream[0],
        query_weight,
        cache_keys[0, :, 0, :].T,
        cache_values[0, :, 0, :].T,
        new_keys[0, :, 0, :],
        new_values[0, :, 0, :],
        out_weight.T.reshape(heads, model // heads, taken),
        norm_gain[None],
        expert_ids[0],
        expert_weights[0],
        gate_weight[0].T,
        up_weight[0].T,
        down_weight[0],
    )
    return mixed[None]


def solution(mesh):
    in_specs = (
        P("seq", "ctx", None),
        P(None, "head"),
        P("seq", "ctx", "head", None),
        P("seq", "ctx", "head", None),
        P("seq", "ctx", "head", None),
        P("seq", "ctx", "head", None),
        P("head", None),
        P(),
        P("seq", "ctx", None),
        P("seq", "ctx", None),
        P(("seq", "ctx"), None, "head"),
        P(("seq", "ctx"), None, "head"),
        P(("seq", "ctx"), "head", None),
    )
    out_specs = P("seq", "ctx", "head")
    return jax.shard_map(body, mesh=mesh, in_specs=in_specs, out_specs=out_specs, check_vma=False)
```

time: 134 us -> 124 us (0.925)
  Pallas kernels: 125 us -> 118 us
  other arithmetic: 2.46 us -> 0 us
  matrix products: 1.63 us -> 0 us
    pallas_call x2 -> x1, Pallas kernels: 125 us -> 118 us  [layer(): pl.pallas_call(layer_kernel, out_shape=jax.ShapeDtypeStruct((count, width...]
    dot_general x1 -> x0, matrix products: 1.63 us -> none  [body(): jnp.dot(tokens, query_weight, preferred_element_type=jnp.float32)]
    concatenate x1 -> x0, other arithmetic: 1.38 us -> none  [body(): jnp.concatenate([fresh_keys, fresh_keys], axis=1)]
    unnamed x19 -> x3, local copies, waits for them, and re-layouts: 4.04 us -> 4.19 us
where the time goes in v3:
time: 124 us; the launch traced here: 123 us
  Pallas kernels  118 us (95%)
  local copies, waits for them, and re-layouts  5.5 us (4%)
    pallas_call x1, Pallas kernels, layer(): pl.pallas_call(layer_kernel, out_shape=jax.ShapeDtypeStruct((count, width...  118 us
    unnamed x3, local copies, waits for them, and re-layouts  4.19 us

profile of v3, /device:TPU:1, one launch (start us, length us, event | category | flops | bytes accessed | tf_op | source)
XLA Modules:
  0.0 123.3 jit_solution(8587690664771945217)
XLA Ops:
  0.0 1.3 %broadcast_in_dim.6.gain_ref = f32[1,2880]{1,0:T(1,128)} reshape(f32[2880]{0:T(1024)} %param.20) | data formatting | bytes 23040 | tf_op jit(solution)/shard_map/broadcast_in_dim | solution.py:733
  1.3 1.4 %copy.14 = s32[1,64,4]{2,1,0:T(8,128)} copy(s32[1,64,4]{1,2,0:T(4,128)} %param.21) | data formatting | bytes 2048 | tf_op args[8]
  2.7 1.4 %copy.15 = f32[1,64,4]{2,1,0:T(8,128)} copy(f32[1,64,4]{1,2,0:T(4,128)} %param.22) | data formatting | bytes 2048 | tf_op args[9]
  4.1 117.8 %shard_map.127 = bf16[64,360]{1,0:T(8,128)(2,1)} custom-call(bf16[64,2880]{1,0:T(8,128)(2,1)} %bitcast.26, bf16[2880,512]{1,0:T(8,128)(2,1)} %qw_hbm.1, bf16[64,2048]{1,0:T(8,128)(2,1)} %bitcast.27, bf16[64,2048]{1,0:T(8,128)(2,1)} %bitcast.28, bf16[64,64]{1,0:T(8,128)(2,1)} %bitcast.32, bf16[64,64]{1,0:T(8,128)(2,1)} %bitcast.33, ...), custom_call_target="tpu_custom_call" | custom-call | tf_op jit(solution)/shard_map/pallas_call | solution.py:636
  121.9 1.4 %copy.17 = bf16[1,64,360]{2,1,0:T(8,128)(2,1)} copy(bf16[1,64,360]{2,1,0:T(8,128)(2,1)} %bitcast.29) | data formatting | bytes 92160

commit v4 on v3

--- a/solution.py
+++ b/solution.py
@@ -27,16 +27,21 @@
     qw_hbm,
     kt_hbm,
     vt_hbm,
-    nk_ref,
-    nv_ref,
+    nk_hbm,
+    nv_hbm,
     wo_hbm,
-    gain_ref,
-    ids_ref,
-    weights_ref,
+    gain_hbm,
+    ids_hbm,
+    weights_hbm,
     gate_hbm,
     up_hbm,
     down_hbm,
     out_ref,
+    nk_ref,
+    nv_ref,
+    gain_ref,
+    ids_ref,
+    weights_ref,
     tok,
     qw,
     vt,
@@ -79,6 +84,7 @@
     final,
     back,
     in_sem,
+    e_sem,
     q_send,
     q_recv,
     o_send,
@@ -129,7 +135,19 @@
         pltpu.make_async_copy(kt_hbm, ko.at[half:pair], in_sem.at[2]),
         pltpu.make_async_copy(vt_hbm, vt, in_sem.at[3]),
     ]
-    for load in [tok_load] + qw_loads + kv_loads:
+    small = [
+        pltpu.make_async_copy(source, target, e_sem.at[i])
+        for i, (source, target) in enumerate(
+            (
+                (nk_hbm, nk_ref),
+                (nv_hbm, nv_ref),
+                (gain_hbm, gain_ref),
+                (ids_hbm, ids_ref),
+                (weights_hbm, weights_ref),
+            )
+        )
+    ]
+    for load in [tok_load] + qw_loads + kv_loads + small:
         load.start()
     wo_copy = pltpu.make_async_copy(wo_hbm, wo, w_sem.at[3])
     loads = [
@@ -153,6 +171,16 @@
 
     ke[half:pair, :] = jnp.zeros((half, cached), bf)
     ko[0:half, :] = jnp.zeros((half, cached), bf)
+    tok_load.wait()
+    query = jnp.zeros((count, qw.shape[1]), f32)
+    for (low_k, high_k), load in zip(spans, qw_loads):
+        load.wait()
+        query = query + jnp.dot(tok[:, low_k:high_k], qw[low_k:high_k, :], preferred_element_type=f32)
+    query = (query.astype(bf).astype(f32) * (1.0 / math.sqrt(half))).astype(bf)
+    for j in range(rows // count):
+        qbuf[0, count * j : count * (j + 1), :] = query[:, pair * j : pair * (j + 1)]
+    for load in kv_loads + small:
+        load.wait()
     low_n = lax.broadcasted_iota(jnp.int32, (count, pair), 1) < half
     nk = nk_ref[...].astype(f32)
     nk = jnp.concatenate([nk, nk], axis=1)
@@ -164,17 +192,6 @@
     vn[count : 2 * count, 0:pair] = jnp.where(low_n, 0.0, nv).astype(bf)
     vn[0:count, pair : 2 * pair] = jnp.where(low_n, 1.0, 0.0).astype(bf)
     vn[count : 2 * count, pair : 2 * pair] = jnp.where(low_n, 0.0, 1.0).astype(bf)
-
-    tok_load.wait()
-    query = jnp.zeros((count, qw.shape[1]), f32)
-    for (low_k, high_k), load in zip(spans, qw_loads):
-        load.wait()
-        query = query + jnp.dot(tok[:, low_k:high_k], qw[low_k:high_k, :], preferred_element_type=f32)
-    query = (query.astype(bf).astype(f32) * (1.0 / math.sqrt(half))).astype(bf)
-    for j in range(rows // count):
-        qbuf[0, count * j : count * (j + 1), :] = query[:, pair * j : pair * (j + 1)]
-    for load in kv_loads:
-        load.wait()
 
     pl.semaphore_wait(barrier, experts - 1 + heads - 1)
     right = lax.rem(place + 1, n)
@@ -268,8 +285,9 @@
         tot = whole[:, pair : 2 * pair]
         obuf[k] = (num / tot).astype(bf)
         turned = (both + jnp.log(tot)).T
-        first = lax.broadcasted_iota(jnp.int32, (8, rows), 0) < 4
-        lbuf[k] = jnp.where(first, turned[0:8, :], turned[half : half + 8, :])
+        for i in range(2):
+            for j in range(2):
+                lbuf[k, 2 * i + j : 2 * i + j + 1, :] = turned[i * half : i * half + 1, j * pair : (j + 1) * pair]
 
         @pl.when(k > 0)
         def _():
@@ -282,35 +300,35 @@
         @pl.when(h == i)
         def _():
             own[...] = tok[:, i * width : (i + 1) * width].astype(f32)
-            gain[...] = gain_ref[:, i * width : (i + 1) * width]
+            gain[...] = gain_ref[i * width : (i + 1) * width].reshape(1, width)
 
     ids = ids_ref[...]
     given = weights_ref[...]
-    index = lax.broadcasted_iota(jnp.int32, (count, experts), 1)
-    named = jnp.zeros((count, experts), f32)
-    amount = jnp.zeros((count, experts), f32)
-    for j in range(ids.shape[1]):
-        hit = ids[:, j : j + 1] == index
+    index = lax.broadcasted_iota(jnp.int32, (experts, count), 0)
+    named = jnp.zeros((experts, count), f32)
+    amount = jnp.zeros((experts, count), f32)
+    for j in range(ids.shape[0]):
+        hit = ids[j : j + 1, :] == index
         named = named + jnp.where(hit, 1.0, 0.0)
-        amount = amount + jnp.where(hit, given[:, j : j + 1], 0.0)
+        amount = amount + jnp.where(hit, given[j : j + 1, :], 0.0)
     before = jnp.where(
-        lax.broadcasted_iota(jnp.int32, (count, count), 1)
-        < lax.broadcasted_iota(jnp.int32, (count, count), 0),
+        lax.broadcasted_iota(jnp.int32, (count, count), 0)
+        < lax.broadcasted_iota(jnp.int32, (count, count), 1),
         1.0,
         0.0,
     ).astype(bf)
-    rank = jnp.dot(before, named.astype(bf), preferred_element_type=f32)
+    rank = jnp.dot(named.astype(bf), before, preferred_element_type=f32)
     key = jnp.where(named > 0.5, rank, 128.0)
     spread = jnp.where(
-        lax.div(lax.broadcasted_iota(jnp.int32, (experts, experts * CAP), 1), CAP)
-        == lax.broadcasted_iota(jnp.int32, (experts, experts * CAP), 0),
+        lax.div(lax.broadcasted_iota(jnp.int32, (experts * CAP, experts), 0), CAP)
+        == lax.broadcasted_iota(jnp.int32, (experts * CAP, experts), 1),
         1.0,
         0.0,
     ).astype(bf)
-    key = jnp.dot(key.astype(bf), spread, preferred_element_type=f32)
-    slot = lax.rem(lax.broadcasted_iota(jnp.int32, (count, experts * CAP), 1), CAP).astype(f32)
+    key = jnp.dot(spread, key.astype(bf), preferred_element_type=f32)
+    slot = lax.rem(lax.broadcasted_iota(jnp.int32, (experts * CAP, count), 0), CAP).astype(f32)
     chosen = key == slot
-    select_s[...] = jnp.where(chosen, 1.0, 0.0).T.astype(bf)
+    select_s[...] = jnp.where(chosen, 1.0, 0.0).astype(bf)
 
     def pieces(x):
         one = x.astype(bf)
@@ -319,8 +337,8 @@
         return one, two, (rest - two.astype(f32)).astype(bf)
 
     for i, piece in enumerate(pieces(amount)):
-        on_slots = jnp.dot(piece, spread, preferred_element_type=f32)
-        factor_s[i] = jnp.where(chosen, on_slots, 0.0).astype(bf)
+        on_slots = jnp.dot(spread, piece, preferred_element_type=f32)
+        factor_s[i] = jnp.where(chosen, on_slots, 0.0).T.astype(bf)
 
     for load in loads:
         load.wait()
@@ -355,22 +373,30 @@
     share = jnp.concatenate([x / whole for x in parts], axis=0)
     share = jnp.concatenate([share, share], axis=0).T
     upper = share.astype(bf).astype(f32)
-    first = lax.broadcasted_iota(jnp.int32, share.shape, 1) < 8 * n
+    first = lax.broadcasted_iota(jnp.int32, share.shape, 1) < 4 * n
     split = jnp.where(first, upper, share - upper).astype(bf)
-    spot = lax.broadcasted_iota(jnp.int32, (16 * n, pair * n), 1)
-    line = lax.broadcasted_iota(jnp.int32, (16 * n, pair * n), 0)
-    wanted = lax.div(spot, pair) * 8 + jnp.where(lax.rem(spot, pair) < half, 0, 4)
-    pick = jnp.where(lax.rem(line, 8 * n) == wanted, 1.0, 0.0).astype(bf)
-    factor = jnp.dot(split, pick, preferred_element_type=f32)
-    attn = jnp.zeros((rows, pair), f32)
-    for k in range(n):
-        attn = attn + factor[:, pair * k : pair * (k + 1)] * rbuf_o[k].astype(f32)
-    attn = attn.astype(bf)
+    spot = lax.broadcasted_iota(jnp.int32, (8 * n, pair * n), 1)
+    line = lax.rem(lax.broadcasted_iota(jnp.int32, (8 * n, pair * n), 0), 4 * n)
+    wanted = lax.div(spot, pair) * 4 + jnp.where(lax.rem(spot, pair) < half, 0, 2)
+    halves = []
+    for j in range(2):
+        pick = jnp.where(line == wanted + j, 1.0, 0.0).astype(bf)
+        factor = jnp.dot(split, pick, preferred_element_type=f32)
+        total = jnp.zeros((pair, pair), f32)
+        for k in range(n):
+            total = total + factor[:, pair * k : pair * (k + 1)] * rbuf_o[k, j * pair : (j + 1) * pair, :].astype(f32)
+        halves.append(total.astype(bf))
+    attn = jnp.concatenate(halves, axis=0)
     flat = jnp.concatenate([attn[count * j : count * (j + 1), :] for j in range(rows // count)], axis=1)
+
+    def peer_at(i):
+        across = jnp.where(i < ring, 1 - col, col)
+        dy = jnp.where(i < ring, 2 + i, i - ring + 1)
+        return across * ring + lax.rem(y + dy, ring)
 
     @pl.loop(0, heads - 1)
     def _(i):
-        there = lax.rem(lane_of + 1 + i, heads)
+        there = peer_at(i)
         part = lax.dot_general(flat, wo[there], NT, preferred_element_type=f32)
         pbuf[i] = part.astype(bf)
         remote(pbuf.at[i], prec.at[i], p_send.at[i], p_recv.at[i], {"head": there}).start()
@@ -378,7 +404,7 @@
     mine = lax.dot_general(flat, wo[lane_of], NT, preferred_element_type=f32)
     total = own[...] + mine
     for i in range(heads - 1):
-        there = lax.rem(lane_of + 1 + i, heads)
+        there = peer_at(i)
         remote(pbuf.at[i], prec.at[i], p_send.at[i], p_recv.at[i], {"head": there}).wait_recv()
         total = total + prec[i].astype(f32)
     resid_s[...] = total
@@ -630,15 +656,20 @@
     block = ctxs * CAP
     bf, f32 = jnp.bfloat16, jnp.float32
     vm = pl.BlockSpec(memory_space=pltpu.VMEM)
-    hbm = pl.BlockSpec(memory_space=pl.ANY)
+    hbm = pl.BlockSpec(memory_space=pltpu.HBM)
     dma = pltpu.SemaphoreType.DMA
     spans = -(-model // DEPTH)
     return pl.pallas_call(
         layer_kernel,
         out_shape=jax.ShapeDtypeStruct((count, width), bf),
-        in_specs=[hbm] * 4 + [vm] * 2 + [hbm] + [vm] * 3 + [hbm] * 3,
+        in_specs=[hbm] * 13,
         out_specs=vm,
         scratch_shapes=[
+            pltpu.VMEM(nk.shape, bf),
+            pltpu.VMEM(nv.shape, bf),
+            pltpu.VMEM(gain.shape, f32),
+            pltpu.VMEM(ids.shape, jnp.int32),
+            pltpu.VMEM(weights.shape, f32),
             pltpu.VMEM((count, model), bf),
             pltpu.VMEM(qw.shape, bf),
             pltpu.VMEM(vt.shape, bf),
@@ -660,9 +691,9 @@
             pltpu.VMEM((rows, pair), bf),
             pltpu.VMEM((rows, 2 * pair), f32),
             pltpu.VMEM((ctxs, rows, pair), bf),
-            pltpu.VMEM((ctxs, 8, rows), f32),
+            pltpu.VMEM((ctxs, 4, pair), f32),
             pltpu.VMEM((ctxs, rows, pair), bf),
-            pltpu.VMEM((ctxs, 8, rows), f32),
+            pltpu.VMEM((ctxs, 4, pair), f32),
             pltpu.VMEM(wo.shape, bf),
             pltpu.VMEM((heads - 1, count, width), bf),
             pltpu.VMEM((heads - 1, count, width), bf),
@@ -681,6 +712,7 @@
             pltpu.VMEM((slots, padded), bf),
             pltpu.VMEM((slots, padded), bf),
             dma((4 + spans,)),
+            dma((5,)),
             dma((ctxs,)),
             dma((ctxs,)),
             dma((ctxs,)),
@@ -700,7 +732,7 @@
             dma((experts,)),
         ],
         compiler_params=pltpu.CompilerParams(
-            collective_id=0, has_side_effects=True, vmem_limit_bytes=60 * 1024 * 1024
+            collective_id=0, has_side_effects=True, vmem_limit_bytes=50 * 1024 * 1024
         ),
     )(tokens, qw, kt, vt, nk, nv, wo, gain, ids, weights, gate, up, down)
 
@@ -730,9 +762,9 @@
         new_keys[0, :, 0, :],
         new_values[0, :, 0, :],
         out_weight.T.reshape(heads, model // heads, taken),
-        norm_gain[None],
-        expert_ids[0],
-        expert_weights[0],
+        norm_gain,
+        expert_ids[0].T,
+        expert_weights[0].T,
         gate_weight[0].T,
         up_weight[0].T,
         down_weight[0],

time: 124 us -> 126 us (1.016)
  local copies, waits for them, and re-layouts: 5.5 us -> 8.61 us
    unnamed x3 -> x19, local copies, waits for them, and re-layouts: 4.19 us -> 8.61 us
    broadcast_in_dim x1 -> x0, local copies, waits for them, and re-layouts: 1.31 us -> none  [body(): norm_gain[None]]
where the time goes in v4:
time: 126 us; the launch traced here: 125 us
  Pallas kernels  117 us (93%)
  local copies, waits for them, and re-layouts  8.61 us (7%)
    pallas_call x1, Pallas kernels, layer(): pl.pallas_call(layer_kernel, out_shape=jax.ShapeDtypeStruct((count, width...  117 us
    unnamed x19, local copies, waits for them, and re-layouts  8.61 us

profile of v4, /device:TPU:1, one launch (start us, length us, event | category | flops | bytes accessed | tf_op | source)
XLA Modules:
  0.0 125.3 jit_solution(18014271974483168231)
XLA Ops:
  0.0 0.0 copy-start
  0.0 1.6 %copy-done = bf16[1,2880,360]{1,2,0:T(8,128)(2,1)S(1)} copy-done((bf16[1,2880,360]{1,2,0:T(8,128)(2,1)S(1)}, bf16[1,2880,360]{1,2,0:T(8,128)(2,1)}, u32[]{:S(2)}) %copy-start) | copy-done | bytes 2073624
  1.6 0.0 copy-start.1
  1.6 1.0 copy-done.1
  2.6 0.0 copy-start.2
  2.6 0.9 copy-done.2
  3.5 0.0 copy-start.3
  3.5 0.9 copy-done.3
  4.5 0.0 copy-start.4
  4.5 0.7 copy-done.4
  5.2 0.0 copy-start.5
  5.2 0.7 copy-done.5
  5.9 0.0 copy-start.6
  5.9 0.7 copy-done.6
  6.6 0.0 copy-start.7
  6.6 0.7 copy-done.7
  7.3 0.0 copy-start.8
  7.3 0.7 copy-done.8
  8.0 116.7 %shard_map.127 = bf16[64,360]{1,0:T(8,128)(2,1)S(1)} custom-call(bf16[64,2880]{1,0:T(8,128)(2,1)S(1)} %bitcast.27, bf16[2880,512]{1,0:T(8,128)(2,1)} %qw_hbm.1, bf16[64,2048]{1,0:T(8,128)(2,1)S(1)} %bitcast.28, bf16[64,2048]{1,0:T(8,128)(2,1)S(1)} %bitcast.29, bf16[64,64]{1,0:T(8,128)(2,1)S(1)} %bitcast.31, bf16[64,64]{1,0:T(8,128)(2,1)S(1)} %bitcast.32, ...), custom_call_target="tpu_custom_call" | custom-call | tf_op jit(solution)/shard_map/pallas_call | solution.py:662
  124.7 0.6 copy.15
Async XLA Ops:
  0.0 1.6 %copy-start = (bf16[1,2880,360]{1,2,0:T(8,128)(2,1)S(1)}, bf16[1,2880,360]{1,2,0:T(8,128)(2,1)}, u32[]{:S(2)}) copy-start(bf16[1,2880,360]{1,2,0:T(8,128)(2,1)} %param.23) | copy-start | bytes 6220804
  1.6 1.0 copy-start.1
  2.6 0.9 copy-start.2
  3.5 0.9 copy-start.3
  4.5 0.7 copy-start.4
  5.2 0.7 copy-start.5
  5.9 0.7 copy-start.6
  6.6 0.7 copy-start.7
  7.3 0.7 copy-start.8

commit v5 on v4

--- a/solution.py
+++ b/solution.py
@@ -256,22 +256,20 @@
         level[...] = both
         p_new[...] = jnp.exp2((s_new[turn] - both) * LOG2E).astype(bf)
 
-        @pl.when(k + 1 < n)
+        @pl.when(turn == 0)
         def _():
-            remote(
-                qbuf.at[k + 1], qbuf.at[k + 1], q_send.at[k + 1], q_recv.at[k + 1], {"ctx": right}
-            ).wait_recv()
-
-            @pl.when(k + 3 < n)
-            def _():
-                onward = lax.rem(place + n + 1 - 2 * lax.rem(k, 2), n)
-                remote(
-                    qbuf.at[k + 1],
-                    qbuf.at[k + 3],
-                    q_send.at[k + 3],
-                    q_recv.at[k + 3],
-                    {"ctx": onward},
-                ).start()
+            for ahead, onward in ((1, right), (2, left)):
+                at = k + ahead
+
+                @pl.when(at < n)
+                def _():
+                    remote(qbuf.at[at], qbuf.at[at], q_send.at[at], q_recv.at[at], {"ctx": right}).wait_recv()
+
+                    @pl.when(at + 2 < n)
+                    def _():
+                        remote(
+                            qbuf.at[at], qbuf.at[at + 2], q_send.at[at + 2], q_recv.at[at + 2], {"ctx": onward}
+                        ).start()
 
         score_even(jnp.minimum(k + 1, n - 1), 1 - turn)
         both = level[...]
@@ -460,15 +458,15 @@
         gather(3, g, 0, below).start()
 
     def stage_b(g):
-        gather(1, g, 0, other).wait_recv()
-        gather(4, g, 1, above).start()
-        gather(5, g, 1, below).start()
         gather(2, g, 0, above).wait_recv()
         gather(3, g, 0, below).wait_recv()
         if g % 2 == 0:
             gather(6, g, 2, above).start()
         else:
             gather(6, g, 3, below).start()
+        gather(1, g, 0, other).wait_recv()
+        gather(4, g, 1, above).start()
+        gather(5, g, 1, below).start()
 
     def stage_c(g):
         gather(6, g, 2, above).wait_recv()
@@ -540,49 +538,40 @@
         sbuf[kind, g] = value.astype(bf)
         scatter(kind, g, target).start()
 
-    @pl.loop(0, GROUPS + 4)
+    @pl.loop(0, GROUPS)
+    def _(g):
+        send(0, g, part(g, head_at(1, 2)), other)
+        send(1, g, part(g, head_at(1, -1)), below)
+        send(2, g, part(g, head_at(1, 1)), above)
+
+    @pl.loop(0, GROUPS + 3)
     def _(t):
         @pl.when(t < GROUPS)
         def _():
             g = t
+            value = part(g, head_at(0, 2)) + got(0, g)
+            send(3, g, value, jnp.where(lax.rem(g, 2) == 0, above, below))
+            value = part(g, other) + got(1, g) + got(2, g)
+            send(4, g, value, other)
+
+        @pl.when((t >= 1) & (t < GROUPS + 1))
+        def _():
+            g = t - 1
             even = lax.rem(g, 2) == 0
-            send(0, g, part(g, head_at(1, 2)), other)
-            send(1, g, part(g, head_at(1, -1)), below)
-            send(2, g, part(g, head_at(1, 1)), above)
 
             @pl.when(even)
             def _():
                 send(5, g, part(g, below), below)
+                send(6, g, part(g, above) + got(3, g), above)
 
             @pl.when(jnp.logical_not(even))
             def _():
                 send(6, g, part(g, above), above)
-
-        @pl.when((t >= 2) & (t < GROUPS + 2))
-        def _():
-            g = t - 2
-            even = lax.rem(g, 2) == 0
-            value = part(g, head_at(0, 2)) + got(0, g)
-            send(3, g, value, jnp.where(even, above, below))
-            value = part(g, other) + got(1, g) + got(2, g)
-            send(4, g, value, other)
-
-        @pl.when((t >= 3) & (t < GROUPS + 3))
+                send(5, g, part(g, below) + got(3, g), below)
+
+        @pl.when(t >= 3)
         def _():
             g = t - 3
-            even = lax.rem(g, 2) == 0
-
-            @pl.when(even)
-            def _():
-                send(6, g, part(g, above) + got(3, g), above)
-
-            @pl.when(jnp.logical_not(even))
-            def _():
-                send(5, g, part(g, below) + got(3, g), below)
-
-        @pl.when(t >= 4)
-        def _():
-            g = t - 4
             value = part(g, h) + got(4, g) + got(5, g) + got(6, g)
             final[rows_of(g)] = value.astype(bf)
             s_to = lax.rem(s + g, seqs)
@@ -656,7 +645,7 @@
     block = ctxs * CAP
     bf, f32 = jnp.bfloat16, jnp.float32
     vm = pl.BlockSpec(memory_space=pltpu.VMEM)
-    hbm = pl.BlockSpec(memory_space=pltpu.HBM)
+    hbm = pl.BlockSpec(memory_space=pl.ANY)
     dma = pltpu.SemaphoreType.DMA
     spans = -(-model // DEPTH)
     return pl.pallas_call(
@@ -732,7 +721,7 @@
             dma((experts,)),
         ],
         compiler_params=pltpu.CompilerParams(
-            collective_id=0, has_side_effects=True, vmem_limit_bytes=50 * 1024 * 1024
+            collective_id=0, has_side_effects=True, vmem_limit_bytes=56 * 1024 * 1024
         ),
     )(tokens, qw, kt, vt, nk, nv, wo, gain, ids, weights, gate, up, down)
 

time: 126 us -> 117 us (0.929)
  local copies, waits for them, and re-layouts: 8.61 us -> 1.42 us
  Pallas kernels: 117 us -> 115 us
    unnamed x19 -> x1, local copies, waits for them, and re-layouts: 8.61 us -> 1.42 us
where the time goes in v5:
time: 117 us
  Pallas kernels  115 us (98%)
  local copies, waits for them, and re-layouts  1.42 us (1%)
    pallas_call x1, Pallas kernels, layer(): pl.pallas_call(layer_kernel, out_shape=jax.ShapeDtypeStruct((count, width...  115 us

profile of v5, /device:TPU:1, one launch (start us, length us, event | category | flops | bytes accessed | tf_op | source)
XLA Modules:
  0.0 116.9 jit_solution(13426557169436007660)
XLA Ops:
  0.0 115.5 %shard_map.127 = bf16[64,360]{1,0:T(8,128)(2,1)} custom-call(bf16[64,2880]{1,0:T(8,128)(2,1)} %bitcast.30, bf16[2880,512]{1,0:T(8,128)(2,1)} %qw_hbm.1, bf16[64,2048]{1,0:T(8,128)(2,1)} %bitcast.31, bf16[64,2048]{1,0:T(8,128)(2,1)} %bitcast.32, bf16[64,64]{1,0:T(8,128)(2,1)} %bitcast.34, bf16[64,64]{1,0:T(8,128)(2,1)} %bitcast.35, ...), custom_call_target="tpu_custom_call" | custom-call | tf_op jit(solution)/shard_map/pallas_call | solution.py:651
  115.5 1.4 %copy.15 = bf16[1,64,360]{2,1,0:T(8,128)(2,1)} copy(bf16[1,64,360]{2,1,0:T(8,128)(2,1)} %bitcast.33) | data formatting | bytes 92160

commit v6 on v5

--- a/solution.py
+++ b/solution.py
@@ -420,14 +420,18 @@
     me = s * ctxs + c
     mine = pl.ds(pl.multiple_of(me * CAP, CAP), CAP)
 
-    @pl.loop(1, experts)
-    def _(step):
+    @pl.loop(0, experts)
+    def _(turn):
+        step = turn - lax.rem(turn, ctxs) + lax.rem(turn + ctxs // 2, ctxs)
         s_to = lax.rem(s + seqs - lax.div(step, ctxs), seqs)
         c_to = lax.rem(c + lax.rem(step, ctxs), ctxs)
         at = pl.ds(pl.multiple_of((s_to * ctxs + c_to) * CAP, CAP), CAP)
-        remote(
-            packed.at[at], xall.at[0, mine], d_send.at[step], d_recv.at[step], {"seq": s_to, "ctx": c_to}
-        ).start()
+
+        @pl.when(step > 0)
+        def _():
+            remote(
+                packed.at[at], xall.at[0, mine], d_send.at[step], d_recv.at[step], {"seq": s_to, "ctx": c_to}
+            ).start()
 
     xall[0, mine] = packed[mine]
 
@@ -508,9 +512,11 @@
         gather(7, g, 6, other).wait_recv()
     absorb(7, 8)
 
-    @pl.loop(0, GROUPS)
-    def _(g):
-        at = pl.ds(pl.multiple_of(g * block, block), block)
+    def rows_back(g):
+        return rows_of(GROUPS - 1 - g)
+
+    def activate(g):
+        at = rows_back(g)
         tile = jnp.zeros((block, 128), f32)
         for k in range(heads):
             tile = tile + xall[k, at, padded - 128 : padded].astype(f32)
@@ -523,7 +529,7 @@
         hidden[at] = (gate * jax.nn.sigmoid(1.702 * gate) * (up + 1.0)).astype(bf)
 
     def part(g, target):
-        return jnp.dot(hidden[rows_of(g)], wdn[target], preferred_element_type=f32)
+        return jnp.dot(hidden[rows_back(g)], wdn[target], preferred_element_type=f32)
 
     def scatter(kind, g, target):
         return remote(
@@ -540,6 +546,7 @@
 
     @pl.loop(0, GROUPS)
     def _(g):
+        activate(g)
         send(0, g, part(g, head_at(1, 2)), other)
         send(1, g, part(g, head_at(1, -1)), below)
         send(2, g, part(g, head_at(1, 1)), above)
@@ -573,14 +580,17 @@
         def _():
             g = t - 3
             value = part(g, h) + got(4, g) + got(5, g) + got(6, g)
-            final[rows_of(g)] = value.astype(bf)
-            s_to = lax.rem(s + g, seqs)
+            final[rows_back(g)] = value.astype(bf)
+            away = GROUPS - 1 - g
+            s_to = lax.rem(s + away, seqs)
 
             @pl.loop(0, ctxs)
-            def _(dc):
-                @pl.when(g * ctxs + dc > 0)
+            def _(order):
+                dc = lax.rem(order + ctxs // 2, ctxs)
+
+                @pl.when(away * ctxs + dc > 0)
                 def _():
-                    step = g * ctxs + dc
+                    step = away * ctxs + dc
                     c_to = lax.rem(c + dc, ctxs)
                     at = pl.ds(pl.multiple_of((s_to * ctxs + c_to) * CAP, CAP), CAP)
                     remote(

time: 117 us -> 114 us (0.974); the launches traced: 117 us -> 113 us
  Pallas kernels: 115 us -> 111 us
    pallas_call x1, Pallas kernels: 115 us -> 111 us  [layer(): pl.pallas_call(layer_kernel, out_shape=jax.ShapeDtypeStruct((count, width...]
where the time goes in v6:
time: 114 us; the launch traced here: 113 us
  Pallas kernels  111 us (97%)
  local copies, waits for them, and re-layouts  1.42 us (1%)
    pallas_call x1, Pallas kernels, layer(): pl.pallas_call(layer_kernel, out_shape=jax.ShapeDtypeStruct((count, width...  111 us

profile of v6, /device:TPU:1, one launch (start us, length us, event | category | flops | bytes accessed | tf_op | source)
XLA Modules:
  0.0 112.6 jit_solution(5881013058946466276)
XLA Ops:
  0.0 111.2 %shard_map.127 = bf16[64,360]{1,0:T(8,128)(2,1)} custom-call(bf16[64,2880]{1,0:T(8,128)(2,1)} %bitcast.30, bf16[2880,512]{1,0:T(8,128)(2,1)} %qw_hbm.1, bf16[64,2048]{1,0:T(8,128)(2,1)} %bitcast.31, bf16[64,2048]{1,0:T(8,128)(2,1)} %bitcast.32, bf16[64,64]{1,0:T(8,128)(2,1)} %bitcast.34, bf16[64,64]{1,0:T(8,128)(2,1)} %bitcast.35, ...), custom_call_target="tpu_custom_call" | custom-call | tf_op jit(solution)/shard_map/pallas_call | solution.py:661
  111.2 1.4 %copy.15 = bf16[1,64,360]{2,1,0:T(8,128)(2,1)} copy(bf16[1,64,360]{2,1,0:T(8,128)(2,1)} %bitcast.33) | data formatting | bytes 92160
